TPU v7x, 32 devices: a whole 2x2x4 slice. The times are simulated.
32 devices in a mesh: row: 4 (over y, x), col: 8 (over z, core).
Axes of the slice: x: 2, y: 2, z: 4, core: 2. Of those that a mesh axis runs over, the one named last changes fastest.
Arguments:
- tokens: bfloat16 [4096, 3584], P(('row', 'col')), may hold values from -6 to 6
- targets: bfloat16 [4096, 3584], P(('row', 'col')), may hold values from -6 to 6
- w_up: bfloat16 [8, 3584, 448], P('col', 'row'), may hold values from -6 to 6
- w_down: bfloat16 [4, 3584, 448], P('row', 'col'), may hold values from -6 to 6
- up_momentum: float32 [8, 3584, 448], P('col', 'row'), may hold values from -2 to 2
- down_momentum: float32 [4, 3584, 448], P('row', 'col'), may hold values from -2 to 2
- member_up: int32 [4, 8], replicated, may hold values from 0 to 1, as said below
- member_down: int32 [4, 8], replicated, may hold values from 0 to 1, as said below
- path_rate: float32 [4, 8], replicated, may hold values from 0.1 to 1
Outputs:
- new_up: bfloat16 [8, 3584, 448], P('col', 'row')
- new_up_momentum: float32 [8, 3584, 448], P('col', 'row')
- new_down: bfloat16 [4, 3584, 448], P('row', 'col')
- new_down_momentum: float32 [4, 3584, 448], P('row', 'col')
Inputs may be any that keep to these rules, and one draw needn't show every extreme that they name: Every column of member_up holds at least one 1. Every row of member_down holds at least one 1.
All inputs are finite; a program needn't handle non-finite values. Where the computation divides by a largest or mean magnitude, that divisor is 1e-20 or more.
Results may differ from a plain program's by a relative error of at most 0.006.
Values may be sent and summed in bfloat16 or wider, within the bound.
No kernel may reach another device: no remote copies, remote signals or barrier semaphores. Data moves between devices by JAX's collectives and lax.ppermute only.
A program may use at most 64 MiB of HBM per device.

v0:
```python
import functools

import jax
import jax.numpy as jnp
from jax import lax
from jax.experimental import pallas as pl
from jax.experimental.pallas import tpu as pltpu
from jax.sharding import PartitionSpec as P


BF16 = jnp.bfloat16
F32 = jnp.float32


def silu_slope(pre):
    sig = jax.nn.sigmoid(pre)
    return sig * (1.0 + pre * (1.0 - sig))


class Ring:
    def __init__(self, axis, size, stride):
        self.axis, self.size, self.stride = axis, size, stride
        self.paired = size & (size - 1) == 0

    def target(self, place, step):
        return place ^ step if self.paired else (place + step) % self.size

    def aim(self, step):
        return self.target(lax.axis_index(self.axis) // self.stride, step)

    def source(self, step):
        if self.paired:
            return lax.axis_index(self.axis) // self.stride ^ step
        return lax.rem(lax.axis_index(self.axis) // self.stride - step + self.size, self.size)

    def back(self, step):
        return step if self.paired else self.size - step

    def permute(self, value, places):
        pairs = []
        for place, there in places:
            for core in range(self.stride):
                pairs.append((place * self.stride + core, there * self.stride + core))
        return lax.ppermute(value, self.axis, pairs)

    def send(self, value, step):
        return self.permute(value, [(p, self.target(p, step)) for p in range(self.size)])


def parity_pair(position, other):
    return 2 * position + (lax.axis_index("col") // 2 + other & 1)


def columns(array, index, width):
    return lax.dynamic_slice_in_dim(array, index * width, width, 1)


def mm(a, b, dims):
    return lax.dot_general(a, b, (dims, ((), ())), preferred_element_type=F32)


def kernel_call(body, outs, args, smem=(), alias=None, scratch=()):
    vmem = pl.BlockSpec(memory_space=pltpu.VMEM)
    specs = [pl.BlockSpec(memory_space=pltpu.SMEM) if i in smem else vmem for i in range(len(args))]
    return pl.pallas_call(
        body,
        out_shape=[jax.ShapeDtypeStruct(*o) for o in outs],
        in_specs=specs,
        out_specs=[vmem] * len(outs),
        scratch_shapes=scratch,
        input_output_aliases=alias or {},
        compiler_params=pltpu.CompilerParams(vmem_limit_bytes=12 * 2**20),
        cost_estimate=pl.CostEstimate(flops=10**8, transcendentals=0, bytes_accessed=2**20),
    )(*args)


def packed_sum(dots, scale, axis, weight, count):
    size = dots.shape[axis]
    square = jnp.sum(dots * dots, axis=axis, keepdims=True) * (1.0 / size)
    spread = jnp.sqrt(square + 1e-05 / scale**2)
    size_of = jnp.abs(dots)
    peak = jnp.max(size_of, axis=axis, keepdims=True)
    largest = peak / (peak + spread) + 1e-06
    inverse = 1.0 / largest
    quant = (dots * pl.reciprocal(size_of + spread) * inverse).astype(BF16).astype(F32)
    return largest * weight / count * quant


def cut_tokens(places, tokens, *refs):
    outs, sems = refs[:-1], refs[-1]
    copies = []
    for i, (place, out) in enumerate(zip(places, outs)):
        width = out.shape[1]
        block = tokens.at[:, pl.ds(pl.multiple_of(place() * width, 128), width)]
        copies.append(pltpu.make_async_copy(block, out, sems.at[i]))
        copies[-1].start()
    for copy in copies:
        copy.wait()


def split(own_pairs, next_pairs, later_pairs, tokens, targets, *outs):
    def cut(ref, place, width):
        return ref[:, pl.ds(pl.multiple_of(place() * width, 128), width)]

    here, following = outs[:2]
    width = here.shape[1] // len(own_pairs)

    def gap(place):
        return cut(tokens, place, width).astype(F32) - cut(targets, place, width).astype(F32)

    for out, places in ((here, own_pairs), (following, next_pairs)):
        for j, place in enumerate(places):
            out[:, j * width : (j + 1) * width] = gap(place).astype(out.dtype)
    for place, out in zip(later_pairs, outs[2:]):
        out[...] = gap(place).astype(out.dtype)


def part_product(module, tokens, out):
    out[...] = mm(module[...], tokens[...], ((1,), (1,))).astype(out.dtype)


def activate(scale, *refs):
    count = len(refs) - (2 if refs[-1].dtype == F32 else 1)
    total = refs[0][...]
    for ref in refs[1:count]:
        total = total + ref[...].astype(F32)
    total = total * scale
    refs[count][...] = jax.nn.silu(total).astype(BF16)
    if count + 2 == len(refs):
        refs[-1][...] = total


def stack_gap(step, own, following, out):
    width = own.shape[1]
    out[0] = own[...]
    out[1] = read_gap(following, (step, width))


def read_gap(ref, where):
    if where is None:
        return ref[...]
    if isinstance(where, int):
        return ref[where]
    step, width = where
    place = lax.axis_index("col") // 4 ^ step
    return ref[:, pl.ds(pl.multiple_of(place * width, 128), width)]


def assemble(half, *refs):
    out = refs[-1]
    rows = refs[0].shape[0]
    place = lax.axis_index("col") // 2
    core = lax.rem(lax.axis_index("col"), 2)
    for s in range(half):
        base = ((place >> 1) ^ s) * (2 * rows)
        mine = pl.multiple_of(base + core * rows, 16)
        other = pl.multiple_of(base + (1 - core) * rows, 16)
        out[pl.ds(mine, rows), :] = refs[2 * s][...]
        out[pl.ds(other, rows), :] = refs[2 * s + 1][...]


def half_slope(scale, gap, act, module, out):
    whole = module[...]
    dy = (gap[...].astype(F32) + mm(act[...], whole, ((0,), (1,))) * scale).astype(BF16)
    out[...] = mm(dy, whole, ((1,), (0,))).astype(out.dtype)


def join_slope(scale, here, there, pre, out):
    total = here[...] + there[...].astype(F32)
    out[...] = (total.T * scale * silu_slope(pre[...])).astype(BF16)


def up_path(first, last, source, scale, *refs):
    refs = list(refs)
    member, rate, tokens, slope = refs[:4]
    rest = refs[4:]
    acc = None if first else rest.pop(0)
    path = source()
    place = lax.axis_index("col")
    count = member[0, place]
    for i in range(1, member.shape[0]):
        count = count + member[i, place]
    weight = member[path, place].astype(F32) * rate[path, place]
    dots = mm(slope[...], tokens[...], ((1,), (0,)))
    total = packed_sum(dots, scale, 0, weight, count.astype(F32))
    if not first:
        total = total + acc[...]
    if last:
        count = (len(rest) - 3) // 2
        momentum, module = rest[:2]
        inputs = rest[2 : 2 + count]
        parts = rest[2 + count : -1]
        rest[-1][...] = total
        moved = 0.9 * momentum[...] + total
        fresh = (module[...].astype(F32) - 0.7 * (total + 0.9 * moved)).astype(BF16)
        for token_part, part in zip(list(inputs) + [tokens], parts):
            part[...] = mm(fresh, token_part[...], ((1,), (1,))).astype(part.dtype)
    else:
        rest[0][...] = total


def outer_update(average, momentum, module, fresh, moved):
    total = average[...]
    moment = 0.9 * momentum[...] + total
    moved[...] = moment
    fresh[...] = (module[...].astype(F32) - 0.7 * (total + 0.9 * moment)).astype(BF16)


def pair_update(mine, other, momentum, module, fresh, moved):
    total = mine[...] + other[...]
    moment = 0.9 * momentum[...] + total
    moved[...] = moment
    fresh[...] = (module[...].astype(F32) - 0.7 * (total + 0.9 * moment)).astype(BF16)


def down_factor(member, rate, path):
    place = lax.axis_index("row")
    count = member[place, 0]
    for i in range(1, member.shape[1]):
        count = count + member[place, i]
    return member[place, path].astype(F32) * rate[place, path], count.astype(F32)


def own_rows(module, half):
    count = module.shape[0] // half
    place = lax.axis_index("col") // 4
    return module[pl.ds(pl.multiple_of(place * count, 16), count), :]


def down_path(first, half, where, source, scale, *refs):
    member, rate, gap, act, module = refs[:5]
    weight, count = down_factor(member, rate, source() * 2 + lax.rem(lax.axis_index("col"), 2))
    hid = act[...].astype(F32).T.astype(BF16)
    dy = (read_gap(gap, where).astype(F32) + mm(hid, own_rows(module, half), ((1,), (1,))) * scale).astype(BF16)
    total = packed_sum(mm(dy, hid, ((0,), (0,))), scale, 1, weight, count)
    if not first:
        total = total + refs[5][...]
    refs[-1][...] = total


def down_last(half, where, source, scale, member, rate, gap, act, module, acc, other, slopes):
    core = lax.rem(lax.axis_index("col"), 2)
    weight, count = down_factor(member, rate, source() * 2 + core)
    hid = act[...].astype(F32).T.astype(BF16)
    dy = read_gap(gap, where).astype(F32) + mm(hid, own_rows(module, half), ((1,), (1,))) * scale
    slopes[...] = dy.T.astype(BF16)
    rows = other.shape[0]
    part = pl.ds(pl.multiple_of((1 - core) * rows, 16), rows)
    total = packed_sum(mm(slopes[part, :], hid, ((1,), (0,))), scale, 1, weight, count)
    other[...] = total + acc[part, :]


def down_mine(source, scale, member, rate, slopes, act, acc, mine):
    core = lax.rem(lax.axis_index("col"), 2)
    weight, count = down_factor(member, rate, source() * 2 + core)
    hid = act[...].astype(F32).T.astype(BF16)
    rows = mine.shape[0]
    part = pl.ds(pl.multiple_of(core * rows, 16), rows)
    total = packed_sum(mm(slopes[part, :], hid, ((1,), (0,))), scale, 1, weight, count)
    mine[...] = total + acc[part, :]


def per_device(
    tokens, targets, w_up, w_down, up_momentum, down_momentum, member_up, member_down, path_rate
):
    tokens_count, width = tokens.shape
    hidden = w_up.shape[2]
    inv_width = width ** (-0.5)
    inv_hidden = hidden ** (-0.5)
    col_count = lax.axis_size("col")
    row = Ring("row", lax.axis_size("row"), 1)
    col = Ring("col", col_count // 2, 2)
    core = lax.rem(lax.axis_index("col"), 2)
    swap = [(i, i ^ 1) for i in range(col_count)]
    row_steps = range(1, row.size)
    col_steps = range(1, col.size)
    up_part = width // row.size
    down_part = width // col.size
    rows = w_down.shape[1]

    def sibling(value):
        return lax.ppermute(value, "col", swap)

    half = col.size // 2

    row_places = [functools.partial(row.aim, s) for s in range(row.size)]
    own_pairs = [functools.partial(parity_pair, j, 0) for j in range(half)]
    next_pairs = [functools.partial(parity_pair, j, 1) for j in range(half)]
    later_pairs = [functools.partial(col.aim, 2 * s) for s in range(half)]
    shapes = [((tokens_count, up_part), BF16)] * row.size
    shapes += [((tokens_count, half * down_part), t) for t in (F32, BF16)]
    shapes += [((tokens_count, down_part), BF16)] * half
    if up_part % 128 or down_part % 128:
        def gap(place):
            return columns(tokens, place(), down_part).astype(F32) - columns(
                targets, place(), down_part
            ).astype(F32)

        cuts = [columns(tokens, place(), up_part) for place in row_places]
        cuts.append(jnp.concatenate([gap(p) for p in own_pairs], axis=1))
        cuts.append(jnp.concatenate([gap(p) for p in next_pairs], axis=1).astype(BF16))
        cuts += [gap(p).astype(BF16) for p in later_pairs]
    else:
        cuts = pl.pallas_call(
            functools.partial(cut_tokens, row_places),
            out_shape=[jax.ShapeDtypeStruct(*o) for o in shapes[: row.size]],
            in_specs=[pl.BlockSpec(memory_space=pl.ANY)],
            out_specs=[pl.BlockSpec(memory_space=pltpu.VMEM)] * row.size,
            scratch_shapes=[pltpu.SemaphoreType.DMA((row.size,))],
            compiler_params=pltpu.CompilerParams(vmem_limit_bytes=2 * 2**20),
            name="cut_tokens",
        )(tokens)
        cuts += kernel_call(
            functools.partial(split, own_pairs, next_pairs, later_pairs),
            shapes[row.size :], [tokens, targets],
        )
    gap_here, gap_next = cuts[row.size : row.size + 2]
    gap_later = cuts[row.size + 2 :]
    inputs = [cuts[0]]
    for s in row_steps:
        inputs.append(row.send(cuts[s], s))

    module_up = w_up[0].T
    flat = (hidden, tokens_count)
    parts = []
    for s in range(row.size):
        (part,) = kernel_call(part_product, [(flat, BF16 if s else F32)], [module_up, inputs[s]])
        if s:
            part = row.send(part, row.back(s))
        parts.append(part)
    act, pre = kernel_call(
        functools.partial(activate, inv_width), [(flat, BF16), (flat, F32)], parts
    )

    blocks = []
    for s in range(half):
        if s:
            block = col.send(w_down[0], 2 * s)
        else:
            block = w_down[0]
        blocks += [block, sibling(block)]
    (module_half,) = kernel_call(
        functools.partial(assemble, half),
        [((half * 2 * rows, hidden), BF16)], blocks,
    )
    gap_next = col.send(gap_next, 1)
    act_next = col.send(act, 1)
    shape = (tokens_count, hidden)
    (there,) = kernel_call(
        functools.partial(half_slope, inv_hidden),
        [(shape, BF16)], [gap_next, act_next, module_half],
    )
    (here,) = kernel_call(
        functools.partial(half_slope, inv_hidden),
        [(shape, F32)], [gap_here, act, module_half],
    )
    there = col.send(there, 1)
    (slope_pre,) = kernel_call(
        functools.partial(join_slope, inv_hidden),
        [((hidden, tokens_count), BF16)], [here, there, pre],
    )

    slopes = [slope_pre] + [row.send(slope_pre, s) for s in row_steps]
    aligned = down_part % 128 == 0
    gap_parts = [(gap_later[0], None), (gap_next, (0, down_part))]
    for s in range(1, half):
        wide = (2, tokens_count, down_part)
        if aligned:
            (both,) = kernel_call(
                functools.partial(stack_gap, s), [(wide, BF16)], [gap_later[s], gap_next],
            )
        else:
            place = lax.axis_index("col") // 4 ^ s
            both = jnp.stack([gap_later[s], columns(gap_next, place, down_part)])
        both = col.send(both, 2 * s)
        gap_parts += [(both, 0), (both, 1)]
    if not aligned:
        gap_parts[1] = (columns(gap_next, lax.axis_index("col") // 4, down_part), None)

    average = None
    for s in range(row.size):
        first, last = s == 0, s == row.size - 1
        args = [member_up, path_rate, inputs[s], slopes[s]]
        alias = {}
        outs = [((hidden, up_part), F32)]
        if not first:
            alias = {len(args): row.size if last else 0}
            args.append(average)
        if last:
            args += [up_momentum[0].T, module_up] + inputs[:-1]
            shape = (hidden, tokens_count)
            outs = [(shape, F32)] + [(shape, BF16)] * (row.size - 1) + outs
        result = kernel_call(
            functools.partial(up_path, first, last, functools.partial(row.source, s), inv_width),
            outs, args, (0, 1), alias,
        )
        average = result[-1]
    fresh, moved = kernel_call(
        outer_update,
        [((hidden, up_part), BF16), ((hidden, up_part), F32)],
        [average, up_momentum[0].T, module_up],
    )

    parts = [result[0]]
    for s in row_steps:
        parts.append(row.send(result[s], row.back(s)))
    (act,) = kernel_call(functools.partial(activate, inv_width), [(flat, BF16)], parts)
    acts = [act] + [col.send(act, s) for s in col_steps]
    sums = None
    for s in range(col.size - 1):
        args = [member_down, path_rate, gap_parts[s][0], acts[s], module_half] + ([sums] if s else [])
        (sums,) = kernel_call(
            functools.partial(down_path, s == 0, half, gap_parts[s][1], functools.partial(col.source, s), inv_hidden),
            [((2 * rows, hidden), F32)], args, (0, 1), {5: 0} if s else {},
        )
    source = functools.partial(col.source, col.size - 1)
    other, slopes_last = kernel_call(
        functools.partial(down_last, half, gap_parts[-1][1], source, inv_hidden),
        [((rows, hidden), F32), ((2 * rows, tokens_count), BF16)],
        [member_down, path_rate, gap_parts[-1][0], acts[-1], module_half, sums],
        (0, 1),
    )
    (mine,) = kernel_call(
        functools.partial(down_mine, source, inv_hidden),
        [((rows, hidden), F32)],
        [member_down, path_rate, slopes_last, acts[-1], sums],
        (0, 1),
    )
    fresh_down, moved_down = kernel_call(
        pair_update,
        [((rows, hidden), BF16), ((rows, hidden), F32)],
        [mine, sibling(other), down_momentum[0], w_down[0]],
    )
    return (fresh.T[None], moved.T[None], fresh_down[None], moved_down[None])


def solution(mesh):
    placed = (
        P(("row", "col"), None),
        P(("row", "col"), None),
        P("col", "row", None),
        P("row", "col", None),
        P("col", "row", None),
        P("row", "col", None),
        P(),
        P(),
        P(),
    )
    return jax.shard_map(
        per_device,
        mesh=mesh,
        in_specs=placed,
        out_specs=(
            P("col", "row", None),
            P("col", "row", None),
            P("row", "col", None),
            P("row", "col", None),
        ),
        check_vma=False,
    )
```

profile of v0, /device:TPU:25, one launch (start us, length us, event | category | flops | bytes accessed | tf_op | source)
XLA Modules:
  0.0 85.7 jit_solution(3614470699082745563)
XLA Ops:
  0.6 0.1 collective-permute-start.7
  0.8 1.2 %copy-done.2 = bf16[128,3584]{1,0:T(8,128)(2,1)S(1)} copy-done((bf16[128,3584]{1,0:T(8,128)(2,1)S(1)}, bf16[128,3584]{1,0:T(8,128)(2,1)}, u32[]{:S(2)}) %copy-start.2) | copy-done | bytes 917528
  2.0 0.1 cut_tokens.1
  2.2 1.3 %collective-permute-start.1 = (bf16[128,896]{1,0:T(8,128)(2,1)S(1)}, bf16[128,896]{1,0:T(8,128)(2,1)S(1)}, u32[]{:S(2)}, u32[]{:S(2)}) collective-permute-start(bf16[128,896]{1,0:T(8,128)(2,1)S(1)} %get-tuple-element.28), channel_id=1, source_target_pairs={{0,8},{8,0},{16,24},{24,16},{1,9},{9,1},{17,25},{25,17},{2,10},{10... | collective-permute-start | bytes 688136 | tf_op jit(solution)/shard_map/ppermute | solution.py:44
  3.4 1.2 %collective-permute-start.3 = (bf16[128,896]{1,0:T(8,128)(2,1)S(1)}, bf16[128,896]{1,0:T(8,128)(2,1)S(1)}, u32[]{:S(2)}, u32[]{:S(2)}) collective-permute-start(bf16[128,896]{1,0:T(8,128)(2,1)S(1)} %get-tuple-element.29), channel_id=1, source_target_pairs={{0,16},{8,24},{16,0},{24,8},{1,17},{9,25},{17,1},{25,9},{2,18},{10... | collective-permute-start | bytes 688136 | tf_op jit(solution)/shard_map/ppermute | solution.py:44
  4.7 0.2 collective-permute-start
  4.9 1.2 %copy-done.3 = bf16[128,3584]{1,0:T(8,128)(2,1)S(1)} copy-done((bf16[128,3584]{1,0:T(8,128)(2,1)S(1)}, bf16[128,3584]{1,0:T(8,128)(2,1)}, u32[]{:S(2)}) %copy-start.3) | copy-done | bytes 917528
  6.0 1.2 %copy-done.5 = bf16[128,3584]{1,0:T(8,128)(2,1)S(1)} copy-done((bf16[128,3584]{1,0:T(8,128)(2,1)S(1)}, bf16[128,3584]{1,0:T(8,128)(2,1)}, u32[]{:S(2)}) %copy-start.5) | copy-done | bytes 917528
  7.2 0.3 shard_map.120
  7.5 0.2 collective-permute-start.9
  7.7 0.8 collective-permute-done.1.tokens.refs_2_.refs_8_
  8.5 3.1 %collective-permute-start.6 = (bf16[448,448]{1,0:T(8,128)(2,1)S(1)}, bf16[448,448]{1,0:T(8,128)(2,1)S(1)}, u32[]{:S(2)}, u32[]{:S(2)}) collective-permute-start(bf16[448,448]{1,0:T(8,128)(2,1)S(1)} %bitcast.25), channel_id=1, source_target_pairs={{0,1},{1,0},{2,3},{3,2},{4,5},{5,4},{6,7},{7,6},{8,9},{9,8},{10,11... | collective-permute-start | bytes 1204232 | tf_op jit(solution)/shard_map/ppermute | solution.py:282
  11.6 12.4 %collective-permute-done.7.refs_2_ = bf16[448,448]{1,0:T(8,128)(2,1)S(1)} collective-permute-done((bf16[448,448]{1,0:T(8,128)(2,1)}, bf16[448,448]{1,0:T(8,128)(2,1)S(1)}, u32[]{:S(2)}, u32[]{:S(2)}) %collective-permute-start.7) | collective-permute-done | bytes 401440 | tf_op jit(solution)/shard_map/ppermute | solution.py:44
  24.0 0.5 collective-permute-start.8
  24.6 0.4 shard_map.122
  25.0 0.0 collective-permute-done.3.tokens.refs_2_.refs_9_
  25.0 1.3 %collective-permute-start.2 = (bf16[448,128]{1,0:T(8,128)(2,1)S(1)}, bf16[448,128]{1,0:T(8,128)(2,1)S(1)}, u32[]{:S(2)}, u32[]{:S(2)}) collective-permute-start(bf16[448,128]{1,0:T(8,128)(2,1)S(1)} %shard_map.122), channel_id=1, source_target_pairs={{0,8},{8,0},{16,24},{24,16},{1,9},{9,1},{17,25},{25,17},{2,10},{10... | collective-permute-start | bytes 344072 | tf_op jit(solution)/shard_map/ppermute | solution.py:44
  26.3 0.4 shard_map.123
  26.7 1.3 %collective-permute-start.4 = (bf16[448,128]{1,0:T(8,128)(2,1)S(1)}, bf16[448,128]{1,0:T(8,128)(2,1)S(1)}, u32[]{:S(2)}, u32[]{:S(2)}) collective-permute-start(bf16[448,128]{1,0:T(8,128)(2,1)S(1)} %shard_map.123), channel_id=1, source_target_pairs={{0,16},{8,24},{16,0},{24,8},{1,17},{9,25},{17,1},{25,9},{2,18},{10... | collective-permute-start | bytes 344072 | tf_op jit(solution)/shard_map/ppermute | solution.py:44
  28.0 0.4 shard_map.124
  28.4 1.4 %collective-permute-done.2.refs_1_ = bf16[448,128]{1,0:T(8,128)(2,1)S(1)} collective-permute-done((bf16[448,128]{1,0:T(8,128)(2,1)S(1)}, bf16[448,128]{1,0:T(8,128)(2,1)S(1)}, u32[]{:S(2)}, u32[]{:S(2)}) %collective-permute-start.2) | collective-permute-done | bytes 114720 | tf_op jit(solution)/shard_map/ppermute | solution.py:44
  29.8 2.2 %collective-permute-start.5 = (bf16[448,128]{1,0:T(8,128)(2,1)S(1)}, bf16[448,128]{1,0:T(8,128)(2,1)S(1)}, u32[]{:S(2)}, u32[]{:S(2)}) collective-permute-start(bf16[448,128]{1,0:T(8,128)(2,1)S(1)} %shard_map.124), channel_id=1, source_target_pairs={{0,24},{8,16},{16,8},{24,0},{1,25},{9,17},{17,9},{25,1},{2,26},{10... | collective-permute-start | bytes 344072 | tf_op jit(solution)/shard_map/ppermute | solution.py:44
  31.9 0.4 shard_map.121.refs_0_
  32.3 2.0 %collective-permute-done.5.refs_3_ = bf16[448,128]{1,0:T(8,128)(2,1)S(1)} collective-permute-done((bf16[448,128]{1,0:T(8,128)(2,1)S(1)}, bf16[448,128]{1,0:T(8,128)(2,1)S(1)}, u32[]{:S(2)}, u32[]{:S(2)}) %collective-permute-start.5) | collective-permute-done | bytes 114720 | tf_op jit(solution)/shard_map/ppermute | solution.py:44
  34.3 0.1 shard_map.125
  34.4 0.1 collective-permute-start.10
  34.5 0.0 collective-permute-done.6.refs_1_
  34.5 0.1 shard_map.126.module.refs_4_
  34.6 3.5 %collective-permute-done.10.act = bf16[448,128]{1,0:T(8,128)(2,1)S(1)} collective-permute-done((bf16[448,128]{1,0:T(8,128)(2,1)S(1)}, bf16[448,128]{1,0:T(8,128)(2,1)S(1)}, u32[]{:S(2)}, u32[]{:S(2)}) %collective-permute-start.10) | collective-permute-done | bytes 114720 | tf_op jit(solution)/shard_map/ppermute | solution.py:44
  38.1 1.0 %shard_map.128 = bf16[128,448]{1,0:T(8,128)(2,1)S(1)} custom-call(bf16[128,1792]{1,0:T(8,128)(2,1)S(1)} %collective-permute-done.9.gap.following.refs_2_, bf16[448,128]{1,0:T(8,128)(2,1)S(1)} %collective-permute-done.10.act, bf16[1792,448]{1,0:T(8,128)(2,1)S(1)} %shard_map.126.module.refs_4_), custom_call_target="tpu_custom_call" | custom-call | flops 100000000 | bytes 1048576 | tf_op jit(solution)/shard_map/pallas_call | solution.py:65
  39.1 0.1 collective-permute-start.11
  39.2 0.3 collective-permute-start.15
  39.6 1.0 %shard_map.127.here = f32[128,448]{1,0:T(8,128)S(1)} custom-call(f32[128,1792]{1,0:T(8,128)S(1)} %get-tuple-element.26.gap, bf16[448,128]{1,0:T(8,128)(2,1)S(1)} %get-tuple-element.30.act, bf16[1792,448]{1,0:T(8,128)(2,1)S(1)} %shard_map.126.module.refs_4_), custom_call_target="tpu_custom_call" | custom-call | flops 100000000 | bytes 1048576 | tf_op jit(solution)/shard_map/pallas_call | solution.py:65
  40.6 3.6 %collective-permute-done.11.there = bf16[128,448]{1,0:T(8,128)(2,1)S(1)} collective-permute-done((bf16[128,448]{1,0:T(8,128)(2,1)S(1)}, bf16[128,448]{1,0:T(8,128)(2,1)S(1)}, u32[]{:S(2)}, u32[]{:S(2)}) %collective-permute-start.11) | collective-permute-done | bytes 114720 | tf_op jit(solution)/shard_map/ppermute | solution.py:44
  44.2 0.1 shard_map.129.refs_3_
  44.4 1.2 %collective-permute-start.14 = (bf16[448,128]{1,0:T(8,128)(2,1)S(1)}, bf16[448,128]{1,0:T(8,128)(2,1)S(1)}, u32[]{:S(2)}, u32[]{:S(2)}) collective-permute-start(bf16[448,128]{1,0:T(8,128)(2,1)S(1)} %shard_map.129.refs_3_), channel_id=1, source_target_pairs={{0,8},{8,0},{16,24},{24,16},{1,9},{9,1},{17,25},{25,17},{2,10},{10... | collective-permute-start | bytes 344072 | tf_op jit(solution)/shard_map/ppermute | solution.py:44
  45.6 1.2 %collective-permute-start.13 = (bf16[448,128]{1,0:T(8,128)(2,1)S(1)}, bf16[448,128]{1,0:T(8,128)(2,1)S(1)}, u32[]{:S(2)}, u32[]{:S(2)}) collective-permute-start(bf16[448,128]{1,0:T(8,128)(2,1)S(1)} %shard_map.129.refs_3_), channel_id=1, source_target_pairs={{0,16},{8,24},{16,0},{24,8},{1,17},{9,25},{17,1},{25,9},{2,18},{10... | collective-permute-start | bytes 344072 | tf_op jit(solution)/shard_map/ppermute | solution.py:44
  46.9 0.2 collective-permute-start.12
  47.1 1.5 %shard_map.130.refs_4_ = f32[448,896]{1,0:T(8,128)S(1)} custom-call(s32[4,8]{1,0:T(4,128)S(1)} %copy-done.9, f32[4,8]{1,0:T(4,128)S(1)} %copy-done.7, bf16[128,896]{1,0:T(8,128)(2,1)S(1)} %get-tuple-element.27.tokens.refs_2_.refs_7_, bf16[448,128]{1,0:T(8,128)(2,1)S(1)} %shard_map.129.refs_3_), custom_call_target="tpu_custom_call" | custom-call | flops 100000000 | bytes 1048576 | tf_op jit(solution)/shard_map/pallas_call | solution.py:65
  48.5 0.0 collective-permute-done.14.refs_3_
  48.6 1.6 %shard_map.131.refs_4_ = f32[448,896]{1,0:T(8,128)S(1)} custom-call(s32[4,8]{1,0:T(4,128)S(1)} %copy-done.9, f32[4,8]{1,0:T(4,128)S(1)} %copy-done.7, bf16[128,896]{1,0:T(8,128)(2,1)S(1)} %collective-permute-done.1.tokens.refs_2_.refs_8_, bf16[448,128]{1,0:T(8,128)(2,1)S(1)} %collective-permute-done.14.refs_3_, ...), custom_call_target="tpu_custom_call", output_to_operand_aliasing={{}: (4, {})} | custom-call | flops 100000000 | bytes 1048576 | tf_op jit(solution)/shard_map/pallas_call | solution.py:65
  50.2 0.0 copy-start.1
  50.2 0.0 collective-permute-done.13.refs_3_
  50.2 1.6 %shard_map.132.refs_4_ = f32[448,896]{1,0:T(8,128)S(1)} custom-call(s32[4,8]{1,0:T(4,128)S(1)} %copy-done.9, f32[4,8]{1,0:T(4,128)S(1)} %copy-done.7, bf16[128,896]{1,0:T(8,128)(2,1)S(1)} %collective-permute-done.3.tokens.refs_2_.refs_9_, bf16[448,128]{1,0:T(8,128)(2,1)S(1)} %collective-permute-done.13.refs_3_, ...), custom_call_target="tpu_custom_call", output_to_operand_aliasing={{}: (4, {})} | custom-call | flops 100000000 | bytes 1048576 | tf_op jit(solution)/shard_map/pallas_call | solution.py:65
  51.9 0.0 copy-start.8
  51.9 2.8 %shard_map.133 = (f32[448,128]{1,0:T(8,128)S(1)}, bf16[448,128]{1,0:T(8,128)(2,1)S(1)}, bf16[448,128]{1,0:T(8,128)(2,1)S(1)}, bf16[448,128]{1,0:T(8,128)(2,1)S(1)}, f32[448,896]{1,0:T(8,128)S(1)}) custom-call(s32[4,8]{1,0:T(4,128)S(1)} %copy-done.9, f32[4,8]{1,0:T(4,128)S(1)} %copy-done.7, ...), custom_call_target="tpu_custom_call", output_to_operand_aliasing={{4}: (4, {})} | custom-call | flops 100000000 | bytes 1048576 | tf_op jit(solution)/shard_map/pallas_call | solution.py:65
  54.8 1.2 %collective-permute-start.16 = (bf16[448,128]{1,0:T(8,128)(2,1)S(1)}, bf16[448,128]{1,0:T(8,128)(2,1)S(1)}, u32[]{:S(2)}, u32[]{:S(2)}) collective-permute-start(bf16[448,128]{1,0:T(8,128)(2,1)S(1)} %get-tuple-element.38), channel_id=1, source_target_pairs={{0,8},{8,0},{16,24},{24,16},{1,9},{9,1},{17,25},{25,17},{2,10},{10... | collective-permute-start | bytes 344072 | tf_op jit(solution)/shard_map/ppermute | solution.py:44
  56.0 1.2 %collective-permute-start.17 = (bf16[448,128]{1,0:T(8,128)(2,1)S(1)}, bf16[448,128]{1,0:T(8,128)(2,1)S(1)}, u32[]{:S(2)}, u32[]{:S(2)}) collective-permute-start(bf16[448,128]{1,0:T(8,128)(2,1)S(1)} %get-tuple-element.39), channel_id=1, source_target_pairs={{0,16},{8,24},{16,0},{24,8},{1,17},{9,25},{17,1},{25,9},{2,18},{10... | collective-permute-start | bytes 344072 | tf_op jit(solution)/shard_map/ppermute | solution.py:44
  57.3 0.6 collective-permute-start.18
  57.8 1.0 %collective-permute-done.16.refs_1_ = bf16[448,128]{1,0:T(8,128)(2,1)S(1)} collective-permute-done((bf16[448,128]{1,0:T(8,128)(2,1)S(1)}, bf16[448,128]{1,0:T(8,128)(2,1)S(1)}, u32[]{:S(2)}, u32[]{:S(2)}) %collective-permute-start.16) | collective-permute-done | bytes 114720 | tf_op jit(solution)/shard_map/ppermute | solution.py:44
  58.8 1.2 %collective-permute-done.17.refs_2_ = bf16[448,128]{1,0:T(8,128)(2,1)S(1)} collective-permute-done((bf16[448,128]{1,0:T(8,128)(2,1)S(1)}, bf16[448,128]{1,0:T(8,128)(2,1)S(1)}, u32[]{:S(2)}, u32[]{:S(2)}) %collective-permute-start.17) | collective-permute-done | bytes 114720 | tf_op jit(solution)/shard_map/ppermute | solution.py:44
  59.9 2.1 %collective-permute-done.18.refs_3_ = bf16[448,128]{1,0:T(8,128)(2,1)S(1)} collective-permute-done((bf16[448,128]{1,0:T(8,128)(2,1)S(1)}, bf16[448,128]{1,0:T(8,128)(2,1)S(1)}, u32[]{:S(2)}, u32[]{:S(2)}) %collective-permute-start.18) | collective-permute-done | bytes 114720 | tf_op jit(solution)/shard_map/ppermute | solution.py:44
  62.1 0.1 shard_map.136.refs_3_
  62.2 0.1 collective-permute-start.21
  62.3 0.1 collective-permute-start.20
  62.3 3.5 %collective-permute-start.19 = (bf16[448,128]{1,0:T(8,128)(2,1)S(1)}, bf16[448,128]{1,0:T(8,128)(2,1)S(1)}, u32[]{:S(2)}, u32[]{:S(2)}) collective-permute-start(bf16[448,128]{1,0:T(8,128)(2,1)S(1)} %shard_map.136.refs_3_), channel_id=1, source_target_pairs={{0,6},{1,7},{2,4},{3,5},{4,2},{5,3},{6,0},{7,1},{8,14},{9,15},{10,... | collective-permute-start | bytes 344072 | tf_op jit(solution)/shard_map/ppermute | solution.py:44
  65.8 2.0 %shard_map.137.refs_5_ = f32[896,448]{1,0:T(8,128)S(1)} custom-call(s32[4,8]{1,0:T(4,128)S(1)} %copy-done.8, f32[4,8]{1,0:T(4,128)S(1)} %copy-done.7, bf16[128,896]{1,0:T(8,128)(2,1)S(1)} %get-tuple-element.41.refs_2_, bf16[448,128]{1,0:T(8,128)(2,1)S(1)} %shard_map.136.refs_3_, bf16[1792,448]{1,0:T(8,128)(2,1)S(1)} %shard_map.126.module.refs_4_), custom_call_target="tpu_custom_call" | custom-call | flops 100000000 | bytes 1048576 | tf_op jit(solution)/shard_map/pallas_call | solution.py:65
  67.9 2.3 %shard_map.138.refs_5_ = f32[896,448]{1,0:T(8,128)S(1)} custom-call(s32[4,8]{1,0:T(4,128)S(1)} %copy-done.8, f32[4,8]{1,0:T(4,128)S(1)} %copy-done.7, bf16[128,1792]{1,0:T(8,128)(2,1)S(1)} %collective-permute-done.9.gap.following.refs_2_, bf16[448,128]{1,0:T(8,128)(2,1)S(1)} %collective-permute-done.21.refs_3_, ...), custom_call_target="tpu_custom_call", output_to_operand_aliasing={{}: (5, {})} | custom-call | flops 100000000 | bytes 1048576 | tf_op jit(solution)/shard_map/pallas_call | solution.py:65
  70.2 2.1 %shard_map.139.acc = f32[896,448]{1,0:T(8,128)S(1)} custom-call(s32[4,8]{1,0:T(4,128)S(1)} %copy-done.8, f32[4,8]{1,0:T(4,128)S(1)} %copy-done.7, bf16[2,128,896]{2,1,0:T(8,128)(2,1)S(1)} %collective-permute-done.15.refs_2_.gap, bf16[448,128]{1,0:T(8,128)(2,1)S(1)} %collective-permute-done.20.refs_3_, ...), custom_call_target="tpu_custom_call", output_to_operand_aliasing={{}: (5, {})} | custom-call | flops 100000000 | bytes 1048576 | tf_op jit(solution)/shard_map/pallas_call | solution.py:65
  72.3 1.7 %shard_map.140 = (f32[448,448]{1,0:T(8,128)S(1)}, bf16[896,128]{1,0:T(8,128)(2,1)S(1)}) custom-call(s32[4,8]{1,0:T(4,128)S(1)} %copy-done.8, f32[4,8]{1,0:T(4,128)S(1)} %copy-done.7, bf16[2,128,896]{2,1,0:T(8,128)(2,1)S(1)} %collective-permute-done.15.refs_2_.gap, bf16[448,128]{1,0:T(8,128)(2,1)S(1)} %collective-permute-done.19.act, ...), custom_call_target="tpu_custom_call" | custom-call | flops 100000000 | bytes 1048576 | tf_op jit(solution)/shard_map/pallas_call | solution.py:65
  74.0 7.2 %collective-permute-start.22 = (f32[448,448]{1,0:T(8,128)S(1)}, f32[448,448]{1,0:T(8,128)S(1)}, u32[]{:S(2)}, u32[]{:S(2)}) collective-permute-start(f32[448,448]{1,0:T(8,128)S(1)} %get-tuple-element.43), channel_id=1, source_target_pairs={{0,1},{1,0},{2,3},{3,2},{4,5},{5,4},{6,7},{7,6},{8,9},{9,8},{10,11... | collective-permute-start | bytes 2408456 | tf_op jit(solution)/shard_map/ppermute | solution.py:282
  81.2 1.7 %shard_map.134 = (bf16[448,896]{1,0:T(8,128)(2,1)}, f32[448,896]{1,0:T(8,128)}) custom-call(f32[448,896]{1,0:T(8,128)S(1)} %get-tuple-element.33.average, f32[448,896]{1,0:T(8,128)S(1)} %bitcast.23, bf16[448,896]{1,0:T(8,128)(2,1)S(1)} %bitcast.21), custom_call_target="tpu_custom_call" | custom-call | flops 100000000 | bytes 1048576 | tf_op jit(solution)/shard_map/pallas_call | solution.py:65
  83.0 1.4 %shard_map.141.mine = f32[448,448]{1,0:T(8,128)S(1)} custom-call(s32[4,8]{1,0:T(4,128)S(1)} %copy-done.8, f32[4,8]{1,0:T(4,128)S(1)} %copy-done.7, bf16[896,128]{1,0:T(8,128)(2,1)S(1)} %get-tuple-element.42.slopes, bf16[448,128]{1,0:T(8,128)(2,1)S(1)} %collective-permute-done.19.act, f32[896,448]{1,0:T(8,128)S(1)} %shard_map.139.acc), custom_call_target="tpu_custom_call" | custom-call | flops 100000000 | bytes 1048576 | tf_op jit(solution)/shard_map/pallas_call | solution.py:65
  84.3 1.3 %shard_map.142 = (bf16[448,448]{1,0:T(8,128)(2,1)}, f32[448,448]{1,0:T(8,128)}) custom-call(f32[448,448]{1,0:T(8,128)S(1)} %shard_map.141.mine, f32[448,448]{1,0:T(8,128)S(1)} %collective-permute-done.22.other, f32[448,448]{1,0:T(8,128)S(1)} %bitcast.28, bf16[448,448]{1,0:T(8,128)(2,1)S(1)} %bitcast.27), custom_call_target="tpu_custom_call" | custom-call | flops 100000000 | bytes 1048576 | tf_op jit(solution)/shard_map/pallas_call | solution.py:65
  (26 shorter events, 0.1 us)
Async XLA Ops:
  0.6 23.9 %copy-start = (bf16[1,896,448]{1,2,0:T(8,128)(2,1)S(1)}, bf16[1,896,448]{1,2,0:T(8,128)(2,1)}, u32[]{:S(2)}) copy-start(bf16[1,896,448]{1,2,0:T(8,128)(2,1)} %param.11) | copy-start | bytes 2408452
  0.6 23.4 %collective-permute-start.7 = (bf16[448,448]{1,0:T(8,128)(2,1)}, bf16[448,448]{1,0:T(8,128)(2,1)S(1)}, u32[]{:S(2)}, u32[]{:S(2)}) collective-permute-start(bf16[448,448]{1,0:T(8,128)(2,1)} %bitcast.24), channel_id=1, source_target_pairs={{0,4},{1,5},{2,6},{3,7},{4,0},{5,1},{6,2},{7,3},{8,12},{9,13},{10,... | collective-permute-start | bytes 1204232 | tf_op jit(solution)/shard_map/ppermute | solution.py:44
  0.8 1.2 %copy-start.2 = (bf16[128,3584]{1,0:T(8,128)(2,1)S(1)}, bf16[128,3584]{1,0:T(8,128)(2,1)}, u32[]{:S(2)}) copy-start(bf16[128,3584]{1,0:T(8,128)(2,1)} %tokens.3) | copy-start | bytes 2752516
  2.2 6.3 %collective-permute-start.1 = (bf16[128,896]{1,0:T(8,128)(2,1)S(1)}, bf16[128,896]{1,0:T(8,128)(2,1)S(1)}, u32[]{:S(2)}, u32[]{:S(2)}) collective-permute-start(bf16[128,896]{1,0:T(8,128)(2,1)S(1)} %get-tuple-element.28), channel_id=1, source_target_pairs={{0,8},{8,0},{16,24},{24,16},{1,9},{9,1},{17,25},{25,17},{2,10},{10... | collective-permute-start | bytes 688136 | tf_op jit(solution)/shard_map/ppermute | solution.py:44
  3.4 21.6 %collective-permute-start.3 = (bf16[128,896]{1,0:T(8,128)(2,1)S(1)}, bf16[128,896]{1,0:T(8,128)(2,1)S(1)}, u32[]{:S(2)}, u32[]{:S(2)}) collective-permute-start(bf16[128,896]{1,0:T(8,128)(2,1)S(1)} %get-tuple-element.29), channel_id=1, source_target_pairs={{0,16},{8,24},{16,0},{24,8},{1,17},{9,25},{17,1},{25,9},{2,18},{10... | collective-permute-start | bytes 688136 | tf_op jit(solution)/shard_map/ppermute | solution.py:44
  4.7 22.0 %collective-permute-start = (bf16[128,896]{1,0:T(8,128)(2,1)S(1)}, bf16[128,896]{1,0:T(8,128)(2,1)S(1)}, u32[]{:S(2)}, u32[]{:S(2)}) collective-permute-start(bf16[128,896]{1,0:T(8,128)(2,1)S(1)} %get-tuple-element.25), channel_id=1, source_target_pairs={{0,24},{8,16},{16,8},{24,0},{1,25},{9,17},{17,9},{25,1},{2,26},{10... | collective-permute-start | bytes 688136 | tf_op jit(solution)/shard_map/ppermute | solution.py:44
  4.9 1.2 %copy-start.3 = (bf16[128,3584]{1,0:T(8,128)(2,1)S(1)}, bf16[128,3584]{1,0:T(8,128)(2,1)}, u32[]{:S(2)}) copy-start(bf16[128,3584]{1,0:T(8,128)(2,1)} %tokens.3) | copy-start | bytes 2752516
  6.0 1.2 %copy-start.5 = (bf16[128,3584]{1,0:T(8,128)(2,1)S(1)}, bf16[128,3584]{1,0:T(8,128)(2,1)}, u32[]{:S(2)}) copy-start(bf16[128,3584]{1,0:T(8,128)(2,1)} %targets.1) | copy-start | bytes 2752516
  7.2 1.3 %copy-start.4 = (bf16[1,448,448]{2,1,0:T(8,128)(2,1)S(1)}, bf16[1,448,448]{2,1,0:T(8,128)(2,1)}, u32[]{:S(2)}) copy-start(bf16[1,448,448]{2,1,0:T(8,128)(2,1)} %param.12) | copy-start | bytes 1204228
  7.5 30.6 %collective-permute-start.9 = (bf16[128,1792]{1,0:T(8,128)(2,1)S(1)}, bf16[128,1792]{1,0:T(8,128)(2,1)S(1)}, u32[]{:S(2)}, u32[]{:S(2)}) collective-permute-start(bf16[128,1792]{1,0:T(8,128)(2,1)S(1)} %get-tuple-element.31), channel_id=1, source_target_pairs={{0,2},{1,3},{2,0},{3,1},{4,6},{5,7},{6,4},{7,5},{8,10},{9,11},{10,... | collective-permute-start | bytes 1376264 | tf_op jit(solution)/shard_map/ppermute | solution.py:44
  8.5 26.0 %collective-permute-start.6 = (bf16[448,448]{1,0:T(8,128)(2,1)S(1)}, bf16[448,448]{1,0:T(8,128)(2,1)S(1)}, u32[]{:S(2)}, u32[]{:S(2)}) collective-permute-start(bf16[448,448]{1,0:T(8,128)(2,1)S(1)} %bitcast.25), channel_id=1, source_target_pairs={{0,1},{1,0},{2,3},{3,2},{4,5},{5,4},{6,7},{7,6},{8,9},{9,8},{10,11... | collective-permute-start | bytes 1204232 | tf_op jit(solution)/shard_map/ppermute | solution.py:282
  24.0 10.5 %collective-permute-start.8 = (bf16[448,448]{1,0:T(8,128)(2,1)S(1)}, bf16[448,448]{1,0:T(8,128)(2,1)S(1)}, u32[]{:S(2)}, u32[]{:S(2)}) collective-permute-start(bf16[448,448]{1,0:T(8,128)(2,1)S(1)} %collective-permute-done.7.refs_2_), channel_id=1, source_target_pairs={{0,1},{1,0},{2,3},{3,2},{4,5},{5,4},{6,7},{7,6},{8,9},{9,8},{10,11... | collective-permute-start | bytes 1204232 | tf_op jit(solution)/shard_map/ppermute | solution.py:282
  25.0 4.8 %collective-permute-start.2 = (bf16[448,128]{1,0:T(8,128)(2,1)S(1)}, bf16[448,128]{1,0:T(8,128)(2,1)S(1)}, u32[]{:S(2)}, u32[]{:S(2)}) collective-permute-start(bf16[448,128]{1,0:T(8,128)(2,1)S(1)} %shard_map.122), channel_id=1, source_target_pairs={{0,8},{8,0},{16,24},{24,16},{1,9},{9,1},{17,25},{25,17},{2,10},{10... | collective-permute-start | bytes 344072 | tf_op jit(solution)/shard_map/ppermute | solution.py:44
  26.7 5.6 %collective-permute-start.4 = (bf16[448,128]{1,0:T(8,128)(2,1)S(1)}, bf16[448,128]{1,0:T(8,128)(2,1)S(1)}, u32[]{:S(2)}, u32[]{:S(2)}) collective-permute-start(bf16[448,128]{1,0:T(8,128)(2,1)S(1)} %shard_map.123), channel_id=1, source_target_pairs={{0,16},{8,24},{16,0},{24,8},{1,17},{9,25},{17,1},{25,9},{2,18},{10... | collective-permute-start | bytes 344072 | tf_op jit(solution)/shard_map/ppermute | solution.py:44
  29.8 4.5 %collective-permute-start.5 = (bf16[448,128]{1,0:T(8,128)(2,1)S(1)}, bf16[448,128]{1,0:T(8,128)(2,1)S(1)}, u32[]{:S(2)}, u32[]{:S(2)}) collective-permute-start(bf16[448,128]{1,0:T(8,128)(2,1)S(1)} %shard_map.124), channel_id=1, source_target_pairs={{0,24},{8,16},{16,8},{24,0},{1,25},{9,17},{17,9},{25,1},{2,26},{10... | collective-permute-start | bytes 344072 | tf_op jit(solution)/shard_map/ppermute | solution.py:44
  34.4 3.7 %collective-permute-start.10 = (bf16[448,128]{1,0:T(8,128)(2,1)S(1)}, bf16[448,128]{1,0:T(8,128)(2,1)S(1)}, u32[]{:S(2)}, u32[]{:S(2)}) collective-permute-start(bf16[448,128]{1,0:T(8,128)(2,1)S(1)} %get-tuple-element.30.act), channel_id=1, source_target_pairs={{0,2},{1,3},{2,0},{3,1},{4,6},{5,7},{6,4},{7,5},{8,10},{9,11},{10,... | collective-permute-start | bytes 344072 | tf_op jit(solution)/shard_map/ppermute | solution.py:44
  39.1 5.1 %collective-permute-start.11 = (bf16[128,448]{1,0:T(8,128)(2,1)S(1)}, bf16[128,448]{1,0:T(8,128)(2,1)S(1)}, u32[]{:S(2)}, u32[]{:S(2)}) collective-permute-start(bf16[128,448]{1,0:T(8,128)(2,1)S(1)} %shard_map.128), channel_id=1, source_target_pairs={{0,2},{1,3},{2,0},{3,1},{4,6},{5,7},{6,4},{7,5},{8,10},{9,11},{10,... | collective-permute-start | bytes 344072 | tf_op jit(solution)/shard_map/ppermute | solution.py:44
  39.2 30.9 %collective-permute-start.15 = (bf16[2,128,896]{2,1,0:T(8,128)(2,1)S(1)}, bf16[2,128,896]{2,1,0:T(8,128)(2,1)S(1)}, u32[]{:S(2)}, u32[]{:S(2)}) collective-permute-start(bf16[2,128,896]{2,1,0:T(8,128)(2,1)S(1)} %shard_map.135), channel_id=1, source_target_pairs={{0,4},{1,5},{2,6},{3,7},{4,0},{5,1},{6,2},{7,3},{8,12},{9,13},{10,... | collective-permute-start | bytes 1376264 | tf_op jit(solution)/shard_map/ppermute | solution.py:44
  39.6 7.5 %copy-start.7 = (f32[4,8]{1,0:T(4,128)S(1)}, f32[4,8]{1,0:T(4,128)}, u32[]{:S(2)}) copy-start(f32[4,8]{1,0:T(4,128)} %rate.3) | copy-start | bytes 388
  39.6 7.5 %copy-start.9 = (s32[4,8]{1,0:T(4,128)S(1)}, s32[4,8]{1,0:T(4,128)}, u32[]{:S(2)}) copy-start(s32[4,8]{1,0:T(4,128)} %refs_0_.10) | copy-start | bytes 388
  44.4 4.2 %collective-permute-start.14 = (bf16[448,128]{1,0:T(8,128)(2,1)S(1)}, bf16[448,128]{1,0:T(8,128)(2,1)S(1)}, u32[]{:S(2)}, u32[]{:S(2)}) collective-permute-start(bf16[448,128]{1,0:T(8,128)(2,1)S(1)} %shard_map.129.refs_3_), channel_id=1, source_target_pairs={{0,8},{8,0},{16,24},{24,16},{1,9},{9,1},{17,25},{25,17},{2,10},{10... | collective-permute-start | bytes 344072 | tf_op jit(solution)/shard_map/ppermute | solution.py:44
  45.6 4.6 %collective-permute-start.13 = (bf16[448,128]{1,0:T(8,128)(2,1)S(1)}, bf16[448,128]{1,0:T(8,128)(2,1)S(1)}, u32[]{:S(2)}, u32[]{:S(2)}) collective-permute-start(bf16[448,128]{1,0:T(8,128)(2,1)S(1)} %shard_map.129.refs_3_), channel_id=1, source_target_pairs={{0,16},{8,24},{16,0},{24,8},{1,17},{9,25},{17,1},{25,9},{2,18},{10... | collective-permute-start | bytes 344072 | tf_op jit(solution)/shard_map/ppermute | solution.py:44
  46.9 5.0 %collective-permute-start.12 = (bf16[448,128]{1,0:T(8,128)(2,1)S(1)}, bf16[448,128]{1,0:T(8,128)(2,1)S(1)}, u32[]{:S(2)}, u32[]{:S(2)}) collective-permute-start(bf16[448,128]{1,0:T(8,128)(2,1)S(1)} %shard_map.129.refs_3_), channel_id=1, source_target_pairs={{0,24},{8,16},{16,8},{24,0},{1,25},{9,17},{17,9},{25,1},{2,26},{10... | collective-permute-start | bytes 344072 | tf_op jit(solution)/shard_map/ppermute | solution.py:44
  50.2 1.7 %copy-start.1 = (f32[1,896,448]{1,2,0:T(8,128)S(1)}, f32[1,896,448]{1,2,0:T(8,128)}, u32[]{:S(2)}) copy-start(f32[1,896,448]{1,2,0:T(8,128)} %param.13) | copy-start | bytes 4816900
  51.9 13.9 %copy-start.8 = (s32[4,8]{1,0:T(4,128)S(1)}, s32[4,8]{1,0:T(4,128)}, u32[]{:S(2)}) copy-start(s32[4,8]{1,0:T(4,128)} %member.3) | copy-start | bytes 388
  54.8 4.0 %collective-permute-start.16 = (bf16[448,128]{1,0:T(8,128)(2,1)S(1)}, bf16[448,128]{1,0:T(8,128)(2,1)S(1)}, u32[]{:S(2)}, u32[]{:S(2)}) collective-permute-start(bf16[448,128]{1,0:T(8,128)(2,1)S(1)} %get-tuple-element.38), channel_id=1, source_target_pairs={{0,8},{8,0},{16,24},{24,16},{1,9},{9,1},{17,25},{25,17},{2,10},{10... | collective-permute-start | bytes 344072 | tf_op jit(solution)/shard_map/ppermute | solution.py:44
  56.0 3.9 %collective-permute-start.17 = (bf16[448,128]{1,0:T(8,128)(2,1)S(1)}, bf16[448,128]{1,0:T(8,128)(2,1)S(1)}, u32[]{:S(2)}, u32[]{:S(2)}) collective-permute-start(bf16[448,128]{1,0:T(8,128)(2,1)S(1)} %get-tuple-element.39), channel_id=1, source_target_pairs={{0,16},{8,24},{16,0},{24,8},{1,17},{9,25},{17,1},{25,9},{2,18},{10... | collective-permute-start | bytes 344072 | tf_op jit(solution)/shard_map/ppermute | solution.py:44
  57.3 4.8 %collective-permute-start.18 = (bf16[448,128]{1,0:T(8,128)(2,1)S(1)}, bf16[448,128]{1,0:T(8,128)(2,1)S(1)}, u32[]{:S(2)}, u32[]{:S(2)}) collective-permute-start(bf16[448,128]{1,0:T(8,128)(2,1)S(1)} %get-tuple-element.40), channel_id=1, source_target_pairs={{0,24},{8,16},{16,8},{24,0},{1,25},{9,17},{17,9},{25,1},{2,26},{10... | collective-permute-start | bytes 344072 | tf_op jit(solution)/shard_map/ppermute | solution.py:44
  62.2 5.7 %collective-permute-start.21 = (bf16[448,128]{1,0:T(8,128)(2,1)S(1)}, bf16[448,128]{1,0:T(8,128)(2,1)S(1)}, u32[]{:S(2)}, u32[]{:S(2)}) collective-permute-start(bf16[448,128]{1,0:T(8,128)(2,1)S(1)} %shard_map.136.refs_3_), channel_id=1, source_target_pairs={{0,2},{1,3},{2,0},{3,1},{4,6},{5,7},{6,4},{7,5},{8,10},{9,11},{10,... | collective-permute-start | bytes 344072 | tf_op jit(solution)/shard_map/ppermute | solution.py:44
  62.3 7.9 %collective-permute-start.20 = (bf16[448,128]{1,0:T(8,128)(2,1)S(1)}, bf16[448,128]{1,0:T(8,128)(2,1)S(1)}, u32[]{:S(2)}, u32[]{:S(2)}) collective-permute-start(bf16[448,128]{1,0:T(8,128)(2,1)S(1)} %shard_map.136.refs_3_), channel_id=1, source_target_pairs={{0,4},{1,5},{2,6},{3,7},{4,0},{5,1},{6,2},{7,3},{8,12},{9,13},{10,... | collective-permute-start | bytes 344072 | tf_op jit(solution)/shard_map/ppermute | solution.py:44
  62.3 10.0 %collective-permute-start.19 = (bf16[448,128]{1,0:T(8,128)(2,1)S(1)}, bf16[448,128]{1,0:T(8,128)(2,1)S(1)}, u32[]{:S(2)}, u32[]{:S(2)}) collective-permute-start(bf16[448,128]{1,0:T(8,128)(2,1)S(1)} %shard_map.136.refs_3_), channel_id=1, source_target_pairs={{0,6},{1,7},{2,4},{3,5},{4,2},{5,3},{6,0},{7,1},{8,14},{9,15},{10,... | collective-permute-start | bytes 344072 | tf_op jit(solution)/shard_map/ppermute | solution.py:44
  74.0 10.3 %collective-permute-start.22 = (f32[448,448]{1,0:T(8,128)S(1)}, f32[448,448]{1,0:T(8,128)S(1)}, u32[]{:S(2)}, u32[]{:S(2)}) collective-permute-start(f32[448,448]{1,0:T(8,128)S(1)} %get-tuple-element.43), channel_id=1, source_target_pairs={{0,1},{1,0},{2,3},{3,2},{4,5},{5,4},{6,7},{7,6},{8,9},{9,8},{10,11... | collective-permute-start | bytes 2408456 | tf_op jit(solution)/shard_map/ppermute | solution.py:282
  83.0 1.4 %copy-start.6 = (f32[1,448,448]{2,1,0:T(8,128)S(1)}, f32[1,448,448]{2,1,0:T(8,128)}, u32[]{:S(2)}) copy-start(f32[1,448,448]{2,1,0:T(8,128)} %param.14) | copy-start | bytes 2408452
where the time goes:
time: 86.6 us; the launch traced here: 85.7 us
  starting transfers between devices  28.4 us (33%)
  waiting for transfers between devices  28 us (32%)
  Pallas kernels  24.7 us (29%)
  local copies, waits for them, and re-layouts  3.64 us (4%)
  between operations  0.97 us (1%)
    ppermute x20, waiting for transfers between devices, permute(): return lax.ppermute(value, self.axis, pairs)  28 us
    pallas_call x23, Pallas kernels, kernel_call(): pl.pallas_call(body, out_shape=[jax.ShapeDtypeStruct(*o) for o in outs],...  24.5 us
    ppermute x20, starting transfers between devices, permute(): return lax.ppermute(value, self.axis, pairs)  17.6 us
    ppermute x3, starting transfers between devices, sibling(): return lax.ppermute(value, 'col', swap)  10.8 us
    unnamed x20, local copies, waits for them, and re-layouts  3.64 us
  transfers between devices with their start and end apart: 23, of which 9 were waited for; matrix products, arithmetic and copies ran while one was open for 0% of the time, Pallas kernels for 24%

commit v1 on v0

--- a/solution.py
+++ b/solution.py
@@ -86,22 +86,17 @@
     return largest * weight / count * quant
 
 
-def cut_tokens(places, tokens, *refs):
-    outs, sems = refs[:-1], refs[-1]
-    copies = []
-    for i, (place, out) in enumerate(zip(places, outs)):
-        width = out.shape[1]
-        block = tokens.at[:, pl.ds(pl.multiple_of(place() * width, 128), width)]
-        copies.append(pltpu.make_async_copy(block, out, sems.at[i]))
-        copies[-1].start()
-    for copy in copies:
-        copy.wait()
+def cut(ref, place, width):
+    return ref[:, pl.ds(pl.multiple_of(place() * width, 128), width)]
+
+
+def cut_tokens(places, tokens, *outs):
+    for place, out in zip(places, outs):
+        out[...] = cut(tokens, place, out.shape[1])
+    outs[-1][...] = tokens[...]
 
 
 def split(own_pairs, next_pairs, later_pairs, tokens, targets, *outs):
-    def cut(ref, place, width):
-        return ref[:, pl.ds(pl.multiple_of(place() * width, 128), width)]
-
     here, following = outs[:2]
     width = here.shape[1] // len(own_pairs)
 
@@ -193,8 +188,11 @@
         rest[-1][...] = total
         moved = 0.9 * momentum[...] + total
         fresh = (module[...].astype(F32) - 0.7 * (total + 0.9 * moved)).astype(BF16)
-        for token_part, part in zip(list(inputs) + [tokens], parts):
-            part[...] = mm(fresh, token_part[...], ((1,), (1,))).astype(part.dtype)
+        together = jnp.concatenate([ref[...] for ref in inputs] + [tokens[...]], axis=0)
+        products = mm(fresh, together, ((1,), (1,)))
+        wide = tokens.shape[0]
+        for i, part in enumerate(parts):
+            part[...] = products[:, i * wide : (i + 1) * wide].astype(part.dtype)
     else:
         rest[0][...] = total
 
@@ -207,7 +205,7 @@
 
 
 def pair_update(mine, other, momentum, module, fresh, moved):
-    total = mine[...] + other[...]
+    total = mine[...] + other[...].astype(F32)
     moment = 0.9 * momentum[...] + total
     moved[...] = moment
     fresh[...] = (module[...].astype(F32) - 0.7 * (total + 0.9 * moment)).astype(BF16)
@@ -247,7 +245,7 @@
     rows = other.shape[0]
     part = pl.ds(pl.multiple_of((1 - core) * rows, 16), rows)
     total = packed_sum(mm(slopes[part, :], hid, ((1,), (0,))), scale, 1, weight, count)
-    other[...] = total + acc[part, :]
+    other[...] = (total + acc[part, :]).astype(other.dtype)
 
 
 def down_mine(source, scale, member, rate, slopes, act, acc, mine):
@@ -301,18 +299,13 @@
         cuts.append(jnp.concatenate([gap(p) for p in next_pairs], axis=1).astype(BF16))
         cuts += [gap(p).astype(BF16) for p in later_pairs]
     else:
-        cuts = pl.pallas_call(
+        *cuts, staged = kernel_call(
             functools.partial(cut_tokens, row_places),
-            out_shape=[jax.ShapeDtypeStruct(*o) for o in shapes[: row.size]],
-            in_specs=[pl.BlockSpec(memory_space=pl.ANY)],
-            out_specs=[pl.BlockSpec(memory_space=pltpu.VMEM)] * row.size,
-            scratch_shapes=[pltpu.SemaphoreType.DMA((row.size,))],
-            compiler_params=pltpu.CompilerParams(vmem_limit_bytes=2 * 2**20),
-            name="cut_tokens",
-        )(tokens)
+            shapes[: row.size] + [(tokens.shape, BF16)], [tokens],
+        )
         cuts += kernel_call(
             functools.partial(split, own_pairs, next_pairs, later_pairs),
-            shapes[row.size :], [tokens, targets],
+            shapes[row.size :], [staged, targets],
         )
     gap_here, gap_next = cuts[row.size : row.size + 2]
     gap_later = cuts[row.size + 2 :]
@@ -416,7 +409,7 @@
     source = functools.partial(col.source, col.size - 1)
     other, slopes_last = kernel_call(
         functools.partial(down_last, half, gap_parts[-1][1], source, inv_hidden),
-        [((rows, hidden), F32), ((2 * rows, tokens_count), BF16)],
+        [((rows, hidden), BF16), ((2 * rows, tokens_count), BF16)],
         [member_down, path_rate, gap_parts[-1][0], acts[-1], module_half, sums],
         (0, 1),
     )

time: 86.6 us -> 86 us (level)
  waiting for transfers between devices: 28 us -> 29.2 us
  local copies, waits for them, and re-layouts: 3.64 us -> 2.46 us
    ppermute x20, waiting for transfers between devices: 28 us -> 29.2 us  [permute(): return lax.ppermute(value, self.axis, pairs)]
    unnamed x20 -> x18, local copies, waits for them, and re-layouts: 3.64 us -> 2.46 us
    pallas_call x23 -> x24, Pallas kernels: 24.5 us -> 24.1 us  [kernel_call(): pl.pallas_call(body, out_shape=[jax.ShapeDtypeStruct(*o) for o in outs],...]
where the time goes in v1:
time: 86 us; the launch traced here: 85.1 us
  waiting for transfers between devices  29.2 us (34%)
  starting transfers between devices  28.4 us (33%)
  Pallas kernels  24.1 us (28%)
  local copies, waits for them, and re-layouts  2.46 us (3%)
  between operations  0.97 us (1%)
    ppermute x20, waiting for transfers between devices, permute(): return lax.ppermute(value, self.axis, pairs)  29.2 us
    pallas_call x24, Pallas kernels, kernel_call(): pl.pallas_call(body, out_shape=[jax.ShapeDtypeStruct(*o) for o in outs],...  24.1 us
    ppermute x20, starting transfers between devices, permute(): return lax.ppermute(value, self.axis, pairs)  17.6 us
    ppermute x3, starting transfers between devices, sibling(): return lax.ppermute(value, 'col', swap)  10.8 us
    unnamed x18, local copies, waits for them, and re-layouts  2.46 us
  transfers between devices with their start and end apart: 23, of which 9 were waited for; matrix products, arithmetic and copies ran while one was open for 0% of the time, Pallas kernels for 24%

profile of v1, /device:TPU:25, one launch (start us, length us, event | category | flops | bytes accessed | tf_op | source)
XLA Modules:
  0.0 85.1 jit_solution(14682332385494139458)
XLA Ops:
  0.7 0.1 collective-permute-start.7
  0.8 1.3 %copy-done.3 = bf16[128,3584]{1,0:T(8,128)(2,1)S(1)} copy-done((bf16[128,3584]{1,0:T(8,128)(2,1)S(1)}, bf16[128,3584]{1,0:T(8,128)(2,1)}, u32[]{:S(2)}) %copy-start.3) | copy-done | bytes 917528
  2.0 0.1 shard_map.120
  2.2 1.3 %collective-permute-start.1 = (bf16[128,896]{1,0:T(8,128)(2,1)S(1)}, bf16[128,896]{1,0:T(8,128)(2,1)S(1)}, u32[]{:S(2)}, u32[]{:S(2)}) collective-permute-start(bf16[128,896]{1,0:T(8,128)(2,1)S(1)} %get-tuple-element.30), channel_id=1, source_target_pairs={{0,8},{8,0},{16,24},{24,16},{1,9},{9,1},{17,25},{25,17},{2,10},{10... | collective-permute-start | bytes 688136 | tf_op jit(solution)/shard_map/ppermute | solution.py:44
  3.4 1.2 %collective-permute-start.3 = (bf16[128,896]{1,0:T(8,128)(2,1)S(1)}, bf16[128,896]{1,0:T(8,128)(2,1)S(1)}, u32[]{:S(2)}, u32[]{:S(2)}) collective-permute-start(bf16[128,896]{1,0:T(8,128)(2,1)S(1)} %get-tuple-element.31), channel_id=1, source_target_pairs={{0,16},{8,24},{16,0},{24,8},{1,17},{9,25},{17,1},{25,9},{2,18},{10... | collective-permute-start | bytes 688136 | tf_op jit(solution)/shard_map/ppermute | solution.py:44
  4.7 0.2 collective-permute-start
  4.9 1.2 %copy-done.4 = bf16[128,3584]{1,0:T(8,128)(2,1)S(1)} copy-done((bf16[128,3584]{1,0:T(8,128)(2,1)S(1)}, bf16[128,3584]{1,0:T(8,128)(2,1)}, u32[]{:S(2)}) %copy-start.4) | copy-done | bytes 917528
  6.1 0.3 shard_map.121
  6.4 0.2 collective-permute-start.9
  6.6 1.9 %collective-permute-done.1.tokens.refs_2_.refs_8_ = bf16[128,896]{1,0:T(8,128)(2,1)S(1)} collective-permute-done((bf16[128,896]{1,0:T(8,128)(2,1)S(1)}, bf16[128,896]{1,0:T(8,128)(2,1)S(1)}, u32[]{:S(2)}, u32[]{:S(2)}) %collective-permute-start.1) | collective-permute-done | bytes 229408 | tf_op jit(solution)/shard_map/ppermute | solution.py:44
  8.5 3.1 %collective-permute-start.6 = (bf16[448,448]{1,0:T(8,128)(2,1)S(1)}, bf16[448,448]{1,0:T(8,128)(2,1)S(1)}, u32[]{:S(2)}, u32[]{:S(2)}) collective-permute-start(bf16[448,448]{1,0:T(8,128)(2,1)S(1)} %bitcast.25), channel_id=1, source_target_pairs={{0,1},{1,0},{2,3},{3,2},{4,5},{5,4},{6,7},{7,6},{8,9},{9,8},{10,11... | collective-permute-start | bytes 1204232 | tf_op jit(solution)/shard_map/ppermute | solution.py:280
  11.6 12.4 %collective-permute-done.7.refs_2_ = bf16[448,448]{1,0:T(8,128)(2,1)S(1)} collective-permute-done((bf16[448,448]{1,0:T(8,128)(2,1)}, bf16[448,448]{1,0:T(8,128)(2,1)S(1)}, u32[]{:S(2)}, u32[]{:S(2)}) %collective-permute-start.7) | collective-permute-done | bytes 401440 | tf_op jit(solution)/shard_map/ppermute | solution.py:44
  24.0 0.5 collective-permute-start.8
  24.6 0.4 shard_map.123
  25.0 0.0 collective-permute-done.3.tokens.refs_2_.refs_9_
  25.0 1.3 %collective-permute-start.2 = (bf16[448,128]{1,0:T(8,128)(2,1)S(1)}, bf16[448,128]{1,0:T(8,128)(2,1)S(1)}, u32[]{:S(2)}, u32[]{:S(2)}) collective-permute-start(bf16[448,128]{1,0:T(8,128)(2,1)S(1)} %shard_map.123), channel_id=1, source_target_pairs={{0,8},{8,0},{16,24},{24,16},{1,9},{9,1},{17,25},{25,17},{2,10},{10... | collective-permute-start | bytes 344072 | tf_op jit(solution)/shard_map/ppermute | solution.py:44
  26.3 0.4 shard_map.124
  26.7 1.3 %collective-permute-start.4 = (bf16[448,128]{1,0:T(8,128)(2,1)S(1)}, bf16[448,128]{1,0:T(8,128)(2,1)S(1)}, u32[]{:S(2)}, u32[]{:S(2)}) collective-permute-start(bf16[448,128]{1,0:T(8,128)(2,1)S(1)} %shard_map.124), channel_id=1, source_target_pairs={{0,16},{8,24},{16,0},{24,8},{1,17},{9,25},{17,1},{25,9},{2,18},{10... | collective-permute-start | bytes 344072 | tf_op jit(solution)/shard_map/ppermute | solution.py:44
  28.0 0.4 shard_map.125
  28.4 1.4 %collective-permute-done.2.refs_1_ = bf16[448,128]{1,0:T(8,128)(2,1)S(1)} collective-permute-done((bf16[448,128]{1,0:T(8,128)(2,1)S(1)}, bf16[448,128]{1,0:T(8,128)(2,1)S(1)}, u32[]{:S(2)}, u32[]{:S(2)}) %collective-permute-start.2) | collective-permute-done | bytes 114720 | tf_op jit(solution)/shard_map/ppermute | solution.py:44
  29.8 2.2 %collective-permute-start.5 = (bf16[448,128]{1,0:T(8,128)(2,1)S(1)}, bf16[448,128]{1,0:T(8,128)(2,1)S(1)}, u32[]{:S(2)}, u32[]{:S(2)}) collective-permute-start(bf16[448,128]{1,0:T(8,128)(2,1)S(1)} %shard_map.125), channel_id=1, source_target_pairs={{0,24},{8,16},{16,8},{24,0},{1,25},{9,17},{17,9},{25,1},{2,26},{10... | collective-permute-start | bytes 344072 | tf_op jit(solution)/shard_map/ppermute | solution.py:44
  31.9 0.4 shard_map.122.refs_0_
  32.3 0.0 collective-permute-done.4.refs_2_
  32.3 2.0 %collective-permute-done.5.refs_3_ = bf16[448,128]{1,0:T(8,128)(2,1)S(1)} collective-permute-done((bf16[448,128]{1,0:T(8,128)(2,1)S(1)}, bf16[448,128]{1,0:T(8,128)(2,1)S(1)}, u32[]{:S(2)}, u32[]{:S(2)}) %collective-permute-start.5) | collective-permute-done | bytes 114720 | tf_op jit(solution)/shard_map/ppermute | solution.py:44
  34.3 0.1 shard_map.126
  34.4 0.1 collective-permute-start.10
  34.5 0.0 collective-permute-done.6.refs_1_
  34.5 0.1 shard_map.127.module.refs_4_
  34.6 3.5 %collective-permute-done.10.act = bf16[448,128]{1,0:T(8,128)(2,1)S(1)} collective-permute-done((bf16[448,128]{1,0:T(8,128)(2,1)S(1)}, bf16[448,128]{1,0:T(8,128)(2,1)S(1)}, u32[]{:S(2)}, u32[]{:S(2)}) %collective-permute-start.10) | collective-permute-done | bytes 114720 | tf_op jit(solution)/shard_map/ppermute | solution.py:44
  38.1 0.0 collective-permute-done.9.gap.following.refs_2_
  38.1 1.0 %shard_map.129 = bf16[128,448]{1,0:T(8,128)(2,1)S(1)} custom-call(bf16[128,1792]{1,0:T(8,128)(2,1)S(1)} %collective-permute-done.9.gap.following.refs_2_, bf16[448,128]{1,0:T(8,128)(2,1)S(1)} %collective-permute-done.10.act, bf16[1792,448]{1,0:T(8,128)(2,1)S(1)} %shard_map.127.module.refs_4_), custom_call_target="tpu_custom_call" | custom-call | flops 100000000 | bytes 1048576 | tf_op jit(solution)/shard_map/pallas_call | solution.py:65
  39.1 0.1 collective-permute-start.11
  39.2 0.3 collective-permute-start.15
  39.6 1.0 %shard_map.128.here = f32[128,448]{1,0:T(8,128)S(1)} custom-call(f32[128,1792]{1,0:T(8,128)S(1)} %get-tuple-element.28.gap, bf16[448,128]{1,0:T(8,128)(2,1)S(1)} %get-tuple-element.32.act, bf16[1792,448]{1,0:T(8,128)(2,1)S(1)} %shard_map.127.module.refs_4_), custom_call_target="tpu_custom_call" | custom-call | flops 100000000 | bytes 1048576 | tf_op jit(solution)/shard_map/pallas_call | solution.py:65
  40.6 3.7 %collective-permute-done.11.there = bf16[128,448]{1,0:T(8,128)(2,1)S(1)} collective-permute-done((bf16[128,448]{1,0:T(8,128)(2,1)S(1)}, bf16[128,448]{1,0:T(8,128)(2,1)S(1)}, u32[]{:S(2)}, u32[]{:S(2)}) %collective-permute-start.11) | collective-permute-done | bytes 114720 | tf_op jit(solution)/shard_map/ppermute | solution.py:44
  44.2 0.1 shard_map.130.refs_3_
  44.4 1.2 %collective-permute-start.14 = (bf16[448,128]{1,0:T(8,128)(2,1)S(1)}, bf16[448,128]{1,0:T(8,128)(2,1)S(1)}, u32[]{:S(2)}, u32[]{:S(2)}) collective-permute-start(bf16[448,128]{1,0:T(8,128)(2,1)S(1)} %shard_map.130.refs_3_), channel_id=1, source_target_pairs={{0,8},{8,0},{16,24},{24,16},{1,9},{9,1},{17,25},{25,17},{2,10},{10... | collective-permute-start | bytes 344072 | tf_op jit(solution)/shard_map/ppermute | solution.py:44
  45.6 1.2 %collective-permute-start.13 = (bf16[448,128]{1,0:T(8,128)(2,1)S(1)}, bf16[448,128]{1,0:T(8,128)(2,1)S(1)}, u32[]{:S(2)}, u32[]{:S(2)}) collective-permute-start(bf16[448,128]{1,0:T(8,128)(2,1)S(1)} %shard_map.130.refs_3_), channel_id=1, source_target_pairs={{0,16},{8,24},{16,0},{24,8},{1,17},{9,25},{17,1},{25,9},{2,18},{10... | collective-permute-start | bytes 344072 | tf_op jit(solution)/shard_map/ppermute | solution.py:44
  46.9 0.2 collective-permute-start.12
  47.1 1.5 %shard_map.131.refs_4_ = f32[448,896]{1,0:T(8,128)S(1)} custom-call(s32[4,8]{1,0:T(4,128)S(1)} %copy-done.8, f32[4,8]{1,0:T(4,128)S(1)} %copy-done.6, bf16[128,896]{1,0:T(8,128)(2,1)S(1)} %get-tuple-element.29.tokens.refs_2_.refs_7_, bf16[448,128]{1,0:T(8,128)(2,1)S(1)} %shard_map.130.refs_3_), custom_call_target="tpu_custom_call" | custom-call | flops 100000000 | bytes 1048576 | tf_op jit(solution)/shard_map/pallas_call | solution.py:65
  48.6 0.0 collective-permute-done.14.refs_3_
  48.6 1.6 %shard_map.132.refs_4_ = f32[448,896]{1,0:T(8,128)S(1)} custom-call(s32[4,8]{1,0:T(4,128)S(1)} %copy-done.8, f32[4,8]{1,0:T(4,128)S(1)} %copy-done.6, bf16[128,896]{1,0:T(8,128)(2,1)S(1)} %collective-permute-done.1.tokens.refs_2_.refs_8_, bf16[448,128]{1,0:T(8,128)(2,1)S(1)} %collective-permute-done.14.refs_3_, ...), custom_call_target="tpu_custom_call", output_to_operand_aliasing={{}: (4, {})} | custom-call | flops 100000000 | bytes 1048576 | tf_op jit(solution)/shard_map/pallas_call | solution.py:65
  50.2 0.0 copy-start.1
  50.2 1.6 %shard_map.133.refs_4_ = f32[448,896]{1,0:T(8,128)S(1)} custom-call(s32[4,8]{1,0:T(4,128)S(1)} %copy-done.8, f32[4,8]{1,0:T(4,128)S(1)} %copy-done.6, bf16[128,896]{1,0:T(8,128)(2,1)S(1)} %collective-permute-done.3.tokens.refs_2_.refs_9_, bf16[448,128]{1,0:T(8,128)(2,1)S(1)} %collective-permute-done.13.refs_3_, ...), custom_call_target="tpu_custom_call", output_to_operand_aliasing={{}: (4, {})} | custom-call | flops 100000000 | bytes 1048576 | tf_op jit(solution)/shard_map/pallas_call | solution.py:65
  51.9 0.0 copy-start.7
  51.9 2.4 %shard_map.134 = (f32[448,128]{1,0:T(8,128)S(1)}, bf16[448,128]{1,0:T(8,128)(2,1)S(1)}, bf16[448,128]{1,0:T(8,128)(2,1)S(1)}, bf16[448,128]{1,0:T(8,128)(2,1)S(1)}, f32[448,896]{1,0:T(8,128)S(1)}) custom-call(s32[4,8]{1,0:T(4,128)S(1)} %copy-done.8, f32[4,8]{1,0:T(4,128)S(1)} %copy-done.6, ...), custom_call_target="tpu_custom_call", output_to_operand_aliasing={{4}: (4, {})} | custom-call | flops 100000000 | bytes 1048576 | tf_op jit(solution)/shard_map/pallas_call | solution.py:65
  54.3 1.3 %collective-permute-start.16 = (bf16[448,128]{1,0:T(8,128)(2,1)S(1)}, bf16[448,128]{1,0:T(8,128)(2,1)S(1)}, u32[]{:S(2)}, u32[]{:S(2)}) collective-permute-start(bf16[448,128]{1,0:T(8,128)(2,1)S(1)} %get-tuple-element.40), channel_id=1, source_target_pairs={{0,8},{8,0},{16,24},{24,16},{1,9},{9,1},{17,25},{25,17},{2,10},{10... | collective-permute-start | bytes 344072 | tf_op jit(solution)/shard_map/ppermute | solution.py:44
  55.5 1.2 %collective-permute-start.17 = (bf16[448,128]{1,0:T(8,128)(2,1)S(1)}, bf16[448,128]{1,0:T(8,128)(2,1)S(1)}, u32[]{:S(2)}, u32[]{:S(2)}) collective-permute-start(bf16[448,128]{1,0:T(8,128)(2,1)S(1)} %get-tuple-element.41), channel_id=1, source_target_pairs={{0,16},{8,24},{16,0},{24,8},{1,17},{9,25},{17,1},{25,9},{2,18},{10... | collective-permute-start | bytes 344072 | tf_op jit(solution)/shard_map/ppermute | solution.py:44
  56.8 0.6 collective-permute-start.18
  57.3 1.0 %collective-permute-done.16.refs_1_ = bf16[448,128]{1,0:T(8,128)(2,1)S(1)} collective-permute-done((bf16[448,128]{1,0:T(8,128)(2,1)S(1)}, bf16[448,128]{1,0:T(8,128)(2,1)S(1)}, u32[]{:S(2)}, u32[]{:S(2)}) %collective-permute-start.16) | collective-permute-done | bytes 114720 | tf_op jit(solution)/shard_map/ppermute | solution.py:44
  58.3 1.2 %collective-permute-done.17.refs_2_ = bf16[448,128]{1,0:T(8,128)(2,1)S(1)} collective-permute-done((bf16[448,128]{1,0:T(8,128)(2,1)S(1)}, bf16[448,128]{1,0:T(8,128)(2,1)S(1)}, u32[]{:S(2)}, u32[]{:S(2)}) %collective-permute-start.17) | collective-permute-done | bytes 114720 | tf_op jit(solution)/shard_map/ppermute | solution.py:44
  59.5 2.1 %collective-permute-done.18.refs_3_ = bf16[448,128]{1,0:T(8,128)(2,1)S(1)} collective-permute-done((bf16[448,128]{1,0:T(8,128)(2,1)S(1)}, bf16[448,128]{1,0:T(8,128)(2,1)S(1)}, u32[]{:S(2)}, u32[]{:S(2)}) %collective-permute-start.18) | collective-permute-done | bytes 114720 | tf_op jit(solution)/shard_map/ppermute | solution.py:44
  61.6 0.1 shard_map.137.refs_3_
  61.7 0.1 collective-permute-start.21
  61.8 0.1 collective-permute-start.20
  61.9 3.5 %collective-permute-start.19 = (bf16[448,128]{1,0:T(8,128)(2,1)S(1)}, bf16[448,128]{1,0:T(8,128)(2,1)S(1)}, u32[]{:S(2)}, u32[]{:S(2)}) collective-permute-start(bf16[448,128]{1,0:T(8,128)(2,1)S(1)} %shard_map.137.refs_3_), channel_id=1, source_target_pairs={{0,6},{1,7},{2,4},{3,5},{4,2},{5,3},{6,0},{7,1},{8,14},{9,15},{10,... | collective-permute-start | bytes 344072 | tf_op jit(solution)/shard_map/ppermute | solution.py:44
  65.3 2.0 %shard_map.138.refs_5_ = f32[896,448]{1,0:T(8,128)S(1)} custom-call(s32[4,8]{1,0:T(4,128)S(1)} %copy-done.7, f32[4,8]{1,0:T(4,128)S(1)} %copy-done.6, bf16[128,896]{1,0:T(8,128)(2,1)S(1)} %get-tuple-element.43.refs_2_, bf16[448,128]{1,0:T(8,128)(2,1)S(1)} %shard_map.137.refs_3_, bf16[1792,448]{1,0:T(8,128)(2,1)S(1)} %shard_map.127.module.refs_4_), custom_call_target="tpu_custom_call" | custom-call | flops 100000000 | bytes 1048576 | tf_op jit(solution)/shard_map/pallas_call | solution.py:65
  67.4 2.3 %shard_map.139.refs_5_ = f32[896,448]{1,0:T(8,128)S(1)} custom-call(s32[4,8]{1,0:T(4,128)S(1)} %copy-done.7, f32[4,8]{1,0:T(4,128)S(1)} %copy-done.6, bf16[128,1792]{1,0:T(8,128)(2,1)S(1)} %collective-permute-done.9.gap.following.refs_2_, bf16[448,128]{1,0:T(8,128)(2,1)S(1)} %collective-permute-done.21.refs_3_, ...), custom_call_target="tpu_custom_call", output_to_operand_aliasing={{}: (5, {})} | custom-call | flops 100000000 | bytes 1048576 | tf_op jit(solution)/shard_map/pallas_call | solution.py:65
  69.7 2.1 %shard_map.140.acc = f32[896,448]{1,0:T(8,128)S(1)} custom-call(s32[4,8]{1,0:T(4,128)S(1)} %copy-done.7, f32[4,8]{1,0:T(4,128)S(1)} %copy-done.6, bf16[2,128,896]{2,1,0:T(8,128)(2,1)S(1)} %collective-permute-done.15.refs_2_.gap, bf16[448,128]{1,0:T(8,128)(2,1)S(1)} %collective-permute-done.20.refs_3_, ...), custom_call_target="tpu_custom_call", output_to_operand_aliasing={{}: (5, {})} | custom-call | flops 100000000 | bytes 1048576 | tf_op jit(solution)/shard_map/pallas_call | solution.py:65
  71.8 1.7 %shard_map.141 = (bf16[448,448]{1,0:T(8,128)(2,1)S(1)}, bf16[896,128]{1,0:T(8,128)(2,1)S(1)}) custom-call(s32[4,8]{1,0:T(4,128)S(1)} %copy-done.7, f32[4,8]{1,0:T(4,128)S(1)} %copy-done.6, bf16[2,128,896]{2,1,0:T(8,128)(2,1)S(1)} %collective-permute-done.15.refs_2_.gap, bf16[448,128]{1,0:T(8,128)(2,1)S(1)} %collective-permute-done.19.act, ...), custom_call_target="tpu_custom_call" | custom-call | flops 100000000 | bytes 1048576 | tf_op jit(solution)/shard_map/pallas_call | solution.py:65
  73.6 7.2 %collective-permute-start.22 = (bf16[448,448]{1,0:T(8,128)(2,1)S(1)}, bf16[448,448]{1,0:T(8,128)(2,1)S(1)}, u32[]{:S(2)}, u32[]{:S(2)}) collective-permute-start(bf16[448,448]{1,0:T(8,128)(2,1)S(1)} %get-tuple-element.45), channel_id=1, source_target_pairs={{0,1},{1,0},{2,3},{3,2},{4,5},{5,4},{6,7},{7,6},{8,9},{9,8},{10,11... | collective-permute-start | bytes 1204232 | tf_op jit(solution)/shard_map/ppermute | solution.py:280
  80.8 1.7 %shard_map.135 = (bf16[448,896]{1,0:T(8,128)(2,1)}, f32[448,896]{1,0:T(8,128)}) custom-call(f32[448,896]{1,0:T(8,128)S(1)} %get-tuple-element.35.average, f32[448,896]{1,0:T(8,128)S(1)} %bitcast.23, bf16[448,896]{1,0:T(8,128)(2,1)S(1)} %bitcast.21), custom_call_target="tpu_custom_call" | custom-call | flops 100000000 | bytes 1048576 | tf_op jit(solution)/shard_map/pallas_call | solution.py:65
  82.5 1.4 %shard_map.142.mine = f32[448,448]{1,0:T(8,128)S(1)} custom-call(s32[4,8]{1,0:T(4,128)S(1)} %copy-done.7, f32[4,8]{1,0:T(4,128)S(1)} %copy-done.6, bf16[896,128]{1,0:T(8,128)(2,1)S(1)} %get-tuple-element.44.slopes, bf16[448,128]{1,0:T(8,128)(2,1)S(1)} %collective-permute-done.19.act, f32[896,448]{1,0:T(8,128)S(1)} %shard_map.140.acc), custom_call_target="tpu_custom_call" | custom-call | flops 100000000 | bytes 1048576 | tf_op jit(solution)/shard_map/pallas_call | solution.py:65
  83.9 1.3 %shard_map.143 = (bf16[448,448]{1,0:T(8,128)(2,1)}, f32[448,448]{1,0:T(8,128)}) custom-call(f32[448,448]{1,0:T(8,128)S(1)} %shard_map.142.mine, bf16[448,448]{1,0:T(8,128)(2,1)S(1)} %collective-permute-done.22.other, f32[448,448]{1,0:T(8,128)S(1)} %bitcast.28, bf16[448,448]{1,0:T(8,128)(2,1)S(1)} %bitcast.27), custom_call_target="tpu_custom_call" | custom-call | flops 100000000 | bytes 1048576 | tf_op jit(solution)/shard_map/pallas_call | solution.py:65
  (24 shorter events, 0.1 us)
Async XLA Ops:
  0.6 7.9 %copy-start.2 = (bf16[1,448,448]{2,1,0:T(8,128)(2,1)S(1)}, bf16[1,448,448]{2,1,0:T(8,128)(2,1)}, u32[]{:S(2)}) copy-start(bf16[1,448,448]{2,1,0:T(8,128)(2,1)} %param.12) | copy-start | bytes 1204228
  0.6 23.9 %copy-start = (bf16[1,896,448]{1,2,0:T(8,128)(2,1)S(1)}, bf16[1,896,448]{1,2,0:T(8,128)(2,1)}, u32[]{:S(2)}) copy-start(bf16[1,896,448]{1,2,0:T(8,128)(2,1)} %param.11) | copy-start | bytes 2408452
  0.7 23.4 %collective-permute-start.7 = (bf16[448,448]{1,0:T(8,128)(2,1)}, bf16[448,448]{1,0:T(8,128)(2,1)S(1)}, u32[]{:S(2)}, u32[]{:S(2)}) collective-permute-start(bf16[448,448]{1,0:T(8,128)(2,1)} %bitcast.24), channel_id=1, source_target_pairs={{0,4},{1,5},{2,6},{3,7},{4,0},{5,1},{6,2},{7,3},{8,12},{9,13},{10,... | collective-permute-start | bytes 1204232 | tf_op jit(solution)/shard_map/ppermute | solution.py:44
  0.8 1.3 %copy-start.3 = (bf16[128,3584]{1,0:T(8,128)(2,1)S(1)}, bf16[128,3584]{1,0:T(8,128)(2,1)}, u32[]{:S(2)}) copy-start(bf16[128,3584]{1,0:T(8,128)(2,1)} %tokens.1) | copy-start | bytes 2752516
  2.2 6.3 %collective-permute-start.1 = (bf16[128,896]{1,0:T(8,128)(2,1)S(1)}, bf16[128,896]{1,0:T(8,128)(2,1)S(1)}, u32[]{:S(2)}, u32[]{:S(2)}) collective-permute-start(bf16[128,896]{1,0:T(8,128)(2,1)S(1)} %get-tuple-element.30), channel_id=1, source_target_pairs={{0,8},{8,0},{16,24},{24,16},{1,9},{9,1},{17,25},{25,17},{2,10},{10... | collective-permute-start | bytes 688136 | tf_op jit(solution)/shard_map/ppermute | solution.py:44
  3.4 21.6 %collective-permute-start.3 = (bf16[128,896]{1,0:T(8,128)(2,1)S(1)}, bf16[128,896]{1,0:T(8,128)(2,1)S(1)}, u32[]{:S(2)}, u32[]{:S(2)}) collective-permute-start(bf16[128,896]{1,0:T(8,128)(2,1)S(1)} %get-tuple-element.31), channel_id=1, source_target_pairs={{0,16},{8,24},{16,0},{24,8},{1,17},{9,25},{17,1},{25,9},{2,18},{10... | collective-permute-start | bytes 688136 | tf_op jit(solution)/shard_map/ppermute | solution.py:44
  4.7 22.0 %collective-permute-start = (bf16[128,896]{1,0:T(8,128)(2,1)S(1)}, bf16[128,896]{1,0:T(8,128)(2,1)S(1)}, u32[]{:S(2)}, u32[]{:S(2)}) collective-permute-start(bf16[128,896]{1,0:T(8,128)(2,1)S(1)} %get-tuple-element.26), channel_id=1, source_target_pairs={{0,24},{8,16},{16,8},{24,0},{1,25},{9,17},{17,9},{25,1},{2,26},{10... | collective-permute-start | bytes 688136 | tf_op jit(solution)/shard_map/ppermute | solution.py:44
  4.9 1.2 %copy-start.4 = (bf16[128,3584]{1,0:T(8,128)(2,1)S(1)}, bf16[128,3584]{1,0:T(8,128)(2,1)}, u32[]{:S(2)}) copy-start(bf16[128,3584]{1,0:T(8,128)(2,1)} %targets.1) | copy-start | bytes 2752516
  6.4 31.8 %collective-permute-start.9 = (bf16[128,1792]{1,0:T(8,128)(2,1)S(1)}, bf16[128,1792]{1,0:T(8,128)(2,1)S(1)}, u32[]{:S(2)}, u32[]{:S(2)}) collective-permute-start(bf16[128,1792]{1,0:T(8,128)(2,1)S(1)} %get-tuple-element.33), channel_id=1, source_target_pairs={{0,2},{1,3},{2,0},{3,1},{4,6},{5,7},{6,4},{7,5},{8,10},{9,11},{10,... | collective-permute-start | bytes 1376264 | tf_op jit(solution)/shard_map/ppermute | solution.py:44
  8.5 26.0 %collective-permute-start.6 = (bf16[448,448]{1,0:T(8,128)(2,1)S(1)}, bf16[448,448]{1,0:T(8,128)(2,1)S(1)}, u32[]{:S(2)}, u32[]{:S(2)}) collective-permute-start(bf16[448,448]{1,0:T(8,128)(2,1)S(1)} %bitcast.25), channel_id=1, source_target_pairs={{0,1},{1,0},{2,3},{3,2},{4,5},{5,4},{6,7},{7,6},{8,9},{9,8},{10,11... | collective-permute-start | bytes 1204232 | tf_op jit(solution)/shard_map/ppermute | solution.py:280
  24.0 10.5 %collective-permute-start.8 = (bf16[448,448]{1,0:T(8,128)(2,1)S(1)}, bf16[448,448]{1,0:T(8,128)(2,1)S(1)}, u32[]{:S(2)}, u32[]{:S(2)}) collective-permute-start(bf16[448,448]{1,0:T(8,128)(2,1)S(1)} %collective-permute-done.7.refs_2_), channel_id=1, source_target_pairs={{0,1},{1,0},{2,3},{3,2},{4,5},{5,4},{6,7},{7,6},{8,9},{9,8},{10,11... | collective-permute-start | bytes 1204232 | tf_op jit(solution)/shard_map/ppermute | solution.py:280
  25.0 4.8 %collective-permute-start.2 = (bf16[448,128]{1,0:T(8,128)(2,1)S(1)}, bf16[448,128]{1,0:T(8,128)(2,1)S(1)}, u32[]{:S(2)}, u32[]{:S(2)}) collective-permute-start(bf16[448,128]{1,0:T(8,128)(2,1)S(1)} %shard_map.123), channel_id=1, source_target_pairs={{0,8},{8,0},{16,24},{24,16},{1,9},{9,1},{17,25},{25,17},{2,10},{10... | collective-permute-start | bytes 344072 | tf_op jit(solution)/shard_map/ppermute | solution.py:44
  26.7 5.6 %collective-permute-start.4 = (bf16[448,128]{1,0:T(8,128)(2,1)S(1)}, bf16[448,128]{1,0:T(8,128)(2,1)S(1)}, u32[]{:S(2)}, u32[]{:S(2)}) collective-permute-start(bf16[448,128]{1,0:T(8,128)(2,1)S(1)} %shard_map.124), channel_id=1, source_target_pairs={{0,16},{8,24},{16,0},{24,8},{1,17},{9,25},{17,1},{25,9},{2,18},{10... | collective-permute-start | bytes 344072 | tf_op jit(solution)/shard_map/ppermute | solution.py:44
  29.8 4.5 %collective-permute-start.5 = (bf16[448,128]{1,0:T(8,128)(2,1)S(1)}, bf16[448,128]{1,0:T(8,128)(2,1)S(1)}, u32[]{:S(2)}, u32[]{:S(2)}) collective-permute-start(bf16[448,128]{1,0:T(8,128)(2,1)S(1)} %shard_map.125), channel_id=1, source_target_pairs={{0,24},{8,16},{16,8},{24,0},{1,25},{9,17},{17,9},{25,1},{2,26},{10... | collective-permute-start | bytes 344072 | tf_op jit(solution)/shard_map/ppermute | solution.py:44
  34.4 3.7 %collective-permute-start.10 = (bf16[448,128]{1,0:T(8,128)(2,1)S(1)}, bf16[448,128]{1,0:T(8,128)(2,1)S(1)}, u32[]{:S(2)}, u32[]{:S(2)}) collective-permute-start(bf16[448,128]{1,0:T(8,128)(2,1)S(1)} %get-tuple-element.32.act), channel_id=1, source_target_pairs={{0,2},{1,3},{2,0},{3,1},{4,6},{5,7},{6,4},{7,5},{8,10},{9,11},{10,... | collective-permute-start | bytes 344072 | tf_op jit(solution)/shard_map/ppermute | solution.py:44
  39.1 5.1 %collective-permute-start.11 = (bf16[128,448]{1,0:T(8,128)(2,1)S(1)}, bf16[128,448]{1,0:T(8,128)(2,1)S(1)}, u32[]{:S(2)}, u32[]{:S(2)}) collective-permute-start(bf16[128,448]{1,0:T(8,128)(2,1)S(1)} %shard_map.129), channel_id=1, source_target_pairs={{0,2},{1,3},{2,0},{3,1},{4,6},{5,7},{6,4},{7,5},{8,10},{9,11},{10,... | collective-permute-start | bytes 344072 | tf_op jit(solution)/shard_map/ppermute | solution.py:44
  39.2 30.4 %collective-permute-start.15 = (bf16[2,128,896]{2,1,0:T(8,128)(2,1)S(1)}, bf16[2,128,896]{2,1,0:T(8,128)(2,1)S(1)}, u32[]{:S(2)}, u32[]{:S(2)}) collective-permute-start(bf16[2,128,896]{2,1,0:T(8,128)(2,1)S(1)} %shard_map.136), channel_id=1, source_target_pairs={{0,4},{1,5},{2,6},{3,7},{4,0},{5,1},{6,2},{7,3},{8,12},{9,13},{10,... | collective-permute-start | bytes 1376264 | tf_op jit(solution)/shard_map/ppermute | solution.py:44
  39.6 7.5 %copy-start.6 = (f32[4,8]{1,0:T(4,128)S(1)}, f32[4,8]{1,0:T(4,128)}, u32[]{:S(2)}) copy-start(f32[4,8]{1,0:T(4,128)} %rate.3) | copy-start | bytes 388
  39.6 7.5 %copy-start.8 = (s32[4,8]{1,0:T(4,128)S(1)}, s32[4,8]{1,0:T(4,128)}, u32[]{:S(2)}) copy-start(s32[4,8]{1,0:T(4,128)} %refs_0_.10) | copy-start | bytes 388
  44.4 4.2 %collective-permute-start.14 = (bf16[448,128]{1,0:T(8,128)(2,1)S(1)}, bf16[448,128]{1,0:T(8,128)(2,1)S(1)}, u32[]{:S(2)}, u32[]{:S(2)}) collective-permute-start(bf16[448,128]{1,0:T(8,128)(2,1)S(1)} %shard_map.130.refs_3_), channel_id=1, source_target_pairs={{0,8},{8,0},{16,24},{24,16},{1,9},{9,1},{17,25},{25,17},{2,10},{10... | collective-permute-start | bytes 344072 | tf_op jit(solution)/shard_map/ppermute | solution.py:44
  45.6 4.6 %collective-permute-start.13 = (bf16[448,128]{1,0:T(8,128)(2,1)S(1)}, bf16[448,128]{1,0:T(8,128)(2,1)S(1)}, u32[]{:S(2)}, u32[]{:S(2)}) collective-permute-start(bf16[448,128]{1,0:T(8,128)(2,1)S(1)} %shard_map.130.refs_3_), channel_id=1, source_target_pairs={{0,16},{8,24},{16,0},{24,8},{1,17},{9,25},{17,1},{25,9},{2,18},{10... | collective-permute-start | bytes 344072 | tf_op jit(solution)/shard_map/ppermute | solution.py:44
  46.9 5.0 %collective-permute-start.12 = (bf16[448,128]{1,0:T(8,128)(2,1)S(1)}, bf16[448,128]{1,0:T(8,128)(2,1)S(1)}, u32[]{:S(2)}, u32[]{:S(2)}) collective-permute-start(bf16[448,128]{1,0:T(8,128)(2,1)S(1)} %shard_map.130.refs_3_), channel_id=1, source_target_pairs={{0,24},{8,16},{16,8},{24,0},{1,25},{9,17},{17,9},{25,1},{2,26},{10... | collective-permute-start | bytes 344072 | tf_op jit(solution)/shard_map/ppermute | solution.py:44
  50.2 1.7 %copy-start.1 = (f32[1,896,448]{1,2,0:T(8,128)S(1)}, f32[1,896,448]{1,2,0:T(8,128)}, u32[]{:S(2)}) copy-start(f32[1,896,448]{1,2,0:T(8,128)} %param.13) | copy-start | bytes 4816900
  51.9 13.4 %copy-start.7 = (s32[4,8]{1,0:T(4,128)S(1)}, s32[4,8]{1,0:T(4,128)}, u32[]{:S(2)}) copy-start(s32[4,8]{1,0:T(4,128)} %member.3) | copy-start | bytes 388
  54.3 4.0 %collective-permute-start.16 = (bf16[448,128]{1,0:T(8,128)(2,1)S(1)}, bf16[448,128]{1,0:T(8,128)(2,1)S(1)}, u32[]{:S(2)}, u32[]{:S(2)}) collective-permute-start(bf16[448,128]{1,0:T(8,128)(2,1)S(1)} %get-tuple-element.40), channel_id=1, source_target_pairs={{0,8},{8,0},{16,24},{24,16},{1,9},{9,1},{17,25},{25,17},{2,10},{10... | collective-permute-start | bytes 344072 | tf_op jit(solution)/shard_map/ppermute | solution.py:44
  55.5 3.9 %collective-permute-start.17 = (bf16[448,128]{1,0:T(8,128)(2,1)S(1)}, bf16[448,128]{1,0:T(8,128)(2,1)S(1)}, u32[]{:S(2)}, u32[]{:S(2)}) collective-permute-start(bf16[448,128]{1,0:T(8,128)(2,1)S(1)} %get-tuple-element.41), channel_id=1, source_target_pairs={{0,16},{8,24},{16,0},{24,8},{1,17},{9,25},{17,1},{25,9},{2,18},{10... | collective-permute-start | bytes 344072 | tf_op jit(solution)/shard_map/ppermute | solution.py:44
  56.8 4.8 %collective-permute-start.18 = (bf16[448,128]{1,0:T(8,128)(2,1)S(1)}, bf16[448,128]{1,0:T(8,128)(2,1)S(1)}, u32[]{:S(2)}, u32[]{:S(2)}) collective-permute-start(bf16[448,128]{1,0:T(8,128)(2,1)S(1)} %get-tuple-element.42), channel_id=1, source_target_pairs={{0,24},{8,16},{16,8},{24,0},{1,25},{9,17},{17,9},{25,1},{2,26},{10... | collective-permute-start | bytes 344072 | tf_op jit(solution)/shard_map/ppermute | solution.py:44
  61.7 5.7 %collective-permute-start.21 = (bf16[448,128]{1,0:T(8,128)(2,1)S(1)}, bf16[448,128]{1,0:T(8,128)(2,1)S(1)}, u32[]{:S(2)}, u32[]{:S(2)}) collective-permute-start(bf16[448,128]{1,0:T(8,128)(2,1)S(1)} %shard_map.137.refs_3_), channel_id=1, source_target_pairs={{0,2},{1,3},{2,0},{3,1},{4,6},{5,7},{6,4},{7,5},{8,10},{9,11},{10,... | collective-permute-start | bytes 344072 | tf_op jit(solution)/shard_map/ppermute | solution.py:44
  61.8 7.9 %collective-permute-start.20 = (bf16[448,128]{1,0:T(8,128)(2,1)S(1)}, bf16[448,128]{1,0:T(8,128)(2,1)S(1)}, u32[]{:S(2)}, u32[]{:S(2)}) collective-permute-start(bf16[448,128]{1,0:T(8,128)(2,1)S(1)} %shard_map.137.refs_3_), channel_id=1, source_target_pairs={{0,4},{1,5},{2,6},{3,7},{4,0},{5,1},{6,2},{7,3},{8,12},{9,13},{10,... | collective-permute-start | bytes 344072 | tf_op jit(solution)/shard_map/ppermute | solution.py:44
  61.9 9.9 %collective-permute-start.19 = (bf16[448,128]{1,0:T(8,128)(2,1)S(1)}, bf16[448,128]{1,0:T(8,128)(2,1)S(1)}, u32[]{:S(2)}, u32[]{:S(2)}) collective-permute-start(bf16[448,128]{1,0:T(8,128)(2,1)S(1)} %shard_map.137.refs_3_), channel_id=1, source_target_pairs={{0,6},{1,7},{2,4},{3,5},{4,2},{5,3},{6,0},{7,1},{8,14},{9,15},{10,... | collective-permute-start | bytes 344072 | tf_op jit(solution)/shard_map/ppermute | solution.py:44
  73.6 10.3 %collective-permute-start.22 = (bf16[448,448]{1,0:T(8,128)(2,1)S(1)}, bf16[448,448]{1,0:T(8,128)(2,1)S(1)}, u32[]{:S(2)}, u32[]{:S(2)}) collective-permute-start(bf16[448,448]{1,0:T(8,128)(2,1)S(1)} %get-tuple-element.45), channel_id=1, source_target_pairs={{0,1},{1,0},{2,3},{3,2},{4,5},{5,4},{6,7},{7,6},{8,9},{9,8},{10,11... | collective-permute-start | bytes 1204232 | tf_op jit(solution)/shard_map/ppermute | solution.py:280
  82.5 1.4 %copy-start.5 = (f32[1,448,448]{2,1,0:T(8,128)S(1)}, f32[1,448,448]{2,1,0:T(8,128)}, u32[]{:S(2)}) copy-start(f32[1,448,448]{2,1,0:T(8,128)} %param.14) | copy-start | bytes 2408452
